TPU v7x, 32 devices: a whole 2x2x4 slice. The times are simulated.
32 devices in a mesh: row: 16 (over z, y, core), col: 2 (over x).
Axes of the slice: x: 2, y: 2, z: 4, core: 2. Of those that a mesh axis runs over, the one named last changes fastest.
Arguments:
- pair_rep: bfloat16 [2048, 2048, 128], P('row', 'col'), may hold values from -6 to 6
- bias_weight: bfloat16 [128, 12], replicated, may hold values from -0.5 to 0.5
- head_weight: float32 [12], replicated, may hold values from -1 to 1
- queries: float32 [192, 2048], P(None, 'row'), may hold values from -48 to 48, as said below
- key_vectors: float32 [192, 2048], P(None, 'col'), may hold values from -48 to 48, as said below
- values: float32 [192, 2048], P(None, 'col'), may hold values from -6 to 6
- query_points: float32 [3, 48, 2048], P(None, None, 'row'), may hold values from -6 to 6
- key_points: float32 [3, 48, 2048], P(None, None, 'col'), may hold values from -6 to 6
- value_points: float32 [3, 96, 2048], P(None, None, 'col'), may hold values from -6 to 6
- rotations: float32 [3, 3, 2048], replicated, may hold values from -1 to 1, as said below
- translations: float32 [3, 2048], replicated, may hold values from -12 to 12
- residue_count: int32 [1], replicated, may hold values from 1024 to 2048
- grad_output: float32 [192, 2048], P(None, 'row'), may hold values from -6 to 6
- grad_points: float32 [3, 96, 2048], P(None, None, 'row'), may hold values from -6 to 6
- grad_pair: bfloat16 [2048, 12, 128], P('row'), may hold values from -2 to 2
Outputs:
- pair_grad: bfloat16 [2048, 2048, 128], P('row', 'col')
- query_grad: float32 [192, 2048], P(None, ('row', 'col'))
- query_point_grad: float32 [3, 48, 2048], P(None, None, ('row', 'col'))
- query_frame_grad: float32 [3, 4, 2048], P(None, None, ('row', 'col'))
- key_grad: float32 [192, 2048], P(None, ('col', 'row'))
- value_grad: float32 [192, 2048], P(None, ('col', 'row'))
- key_point_grad: float32 [3, 48, 2048], P(None, None, ('col', 'row'))
- value_point_grad: float32 [3, 96, 2048], P(None, None, ('col', 'row'))
- key_frame_grad: float32 [3, 4, 2048], P(None, None, ('col', 'row'))
- bias_weight_grad: float32 [128, 12], replicated
- head_weight_grad: float32 [12], replicated
Inputs may be any that keep to these rules, and one draw needn't show every extreme that they name: `queries`: entries of order one, except a few residues whose vectors are much larger. `key_vectors`: entries of order one, except a few residues whose vectors are much larger. `rotations`: each residue's 3 x 3 matrix is a rotation: orthonormal with determinant one.
All inputs are finite; a program needn't handle non-finite values.
Results may differ from a plain program's by a relative error of at most 0.0049.
Values sent between devices are 32-bit elements; how exact they have to be, the bound alone decides.
A program may use at most 256 MiB of HBM per device.

v0:
```python
import functools
import math

import jax
import jax.numpy as jnp
from jax import lax
from jax.experimental import pallas as pl
from jax.experimental.pallas import tpu as pltpu
from jax.sharding import PartitionSpec as P

F32 = jnp.float32
BF16 = jnp.bfloat16
PAD = 16
VMEM_LIMIT = 60 * 1024 * 1024


def dot(a, b, dims):
    return lax.dot_general(a, b, (dims, ((), ())), preferred_element_type=F32)


TN = ((0,), (0,))
NT = ((1,), (1,))
NN = ((1,), (0,))


def split2(x):
    hi = x.astype(BF16)
    return hi, (x - hi.astype(F32)).astype(BF16)


def split3(x):
    hi = x.astype(BF16)
    rest = x - hi.astype(F32)
    mid = rest.astype(BF16)
    return hi, mid, (rest - mid.astype(F32)).astype(BF16)


def forward_kernel(
    heads, block, scale, limit_ref, pair, bias_w, gpair, qcat, kcat, gcat, vcat,
    e_out, d_out, stat_out, lbase, dbase, rows_buf,
):
    step = pl.program_id(0)

    @pl.when(step == 0)
    def _():
        def head(h, carry):
            q0, q1, q2 = split3(qcat[h])
            k0, k1, k2 = split3(kcat[h])
            lbase[h] = dot(
                jnp.concatenate([q0, q0, q1, q0, q2, q1], 0),
                jnp.concatenate([k0, k1, k0, k2, k0, k1], 0),
                TN,
            )
            g0, g1 = split2(gcat[h])
            v0, v1 = split2(vcat[h])
            dbase[h] = dot(
                jnp.concatenate([g0, g0, g1], 0), jnp.concatenate([v0, v1, v0], 0), TN
            )
            return carry

        lax.fori_loop(0, heads, head, 0)

    for r in range(block):
        w = jnp.concatenate([bias_w[...], gpair[r]], 0)
        rows_buf[r] = dot(w, pair[r], NT)
    cols = pair.shape[1]
    rows = pl.ds(pl.multiple_of(step * block, block), block)
    valid = lax.broadcasted_iota(jnp.int32, (block, cols), 1) < limit_ref[0]
    lane = lax.broadcasted_iota(jnp.int32, (block, 128), 1)
    packed = jnp.ones((block, 128), F32)
    for h in range(heads):
        logit = lbase[h, rows, :] + scale * rows_buf[:, h, :]
        logit = jnp.where(valid, logit, F32(-1000000000.0))
        peak = jnp.max(logit, axis=1, keepdims=True)
        e = jnp.exp(logit - peak)
        d = dbase[h, rows, :] + rows_buf[:, PAD + h, :]
        e_out[h] = e
        d_out[h] = d
        packed = jnp.where(lane == h, peak, packed)
        packed = jnp.where(lane == PAD + h, jnp.sum(e, axis=1, keepdims=True), packed)
        packed = jnp.where(lane == 2 * PAD + h, jnp.sum(e * d, axis=1, keepdims=True), packed)
    stat_out[...] = packed


def merged(stats, own):
    peers = stats.shape[0]
    top = stats[0]
    for c in range(1, peers):
        top = jnp.maximum(top, stats[c])
    total = jnp.zeros_like(top)
    upper = jnp.zeros_like(top)
    for c in range(peers):
        f = jnp.exp(stats[c] - top)
        total = total + pltpu.roll(stats[c], 128 - PAD, 1) * f
        upper = upper + pltpu.roll(stats[c], 128 - 2 * PAD, 1) * f
    return jnp.exp(own - top) / total, upper / total


def sums_kernel(
    nq, nv, vwidth, e_in, d_in, stats, own, qcat, kcat, gcat, vcat, key_out, query_out
):
    h = pl.program_id(0)
    factor, delta = merged(stats, own[...])
    mine = lax.broadcasted_iota(jnp.int32, factor.shape, 1) == h
    pick = lambda x: jnp.sum(jnp.where(mine, x, 0.0), axis=1, keepdims=True)
    att = e_in[0] * pick(factor)
    dl = att * (d_in[0] - pick(delta))
    a0, a1 = split2(att)
    d0, d1 = split2(dl)
    q = jnp.concatenate(split2(qcat[0]), 0)
    k = jnp.concatenate(split2(kcat[0]), 0)
    g = jnp.concatenate(split2(gcat[0]), 0)
    v = jnp.concatenate(split2(vcat[0]), 0)
    kk = dot(q, d0, NN) + dot(q, d1, NN)
    key_out[0, :nq, :] = kk[:nq] + kk[nq:]
    vv = dot(g, a0, NN) + dot(g, a1, NN)
    half = g.shape[0] // 2
    key_out[0, nq:, :] = vv[:nv] + vv[half : half + nv]
    qq = dot(k, d0, NT) + dot(k, d1, NT)
    query_out[0, :nq, :] = qq[:nq] + qq[nq:]
    oo = dot(v, a0, NT) + dot(v, a1, NT)
    query_out[0, nq:, :] = oo[vwidth:nv] + oo[half + vwidth : half + nv]


def pair_kernel(
    heads, block, pair, e_in, d_in, stats, own, scaled, gpair, pg_out, w_out, rows_buf
):
    @pl.when(pl.program_id(0) == 0)
    def _():
        rows_buf[...] = jnp.zeros_like(rows_buf)
        w_out[...] = jnp.zeros_like(w_out)

    factor, delta = merged(stats, own[...])
    w_hi, w_lo = split2(scaled[...])
    for h in range(heads):
        att = e_in[h] * factor[:, h : h + 1]
        rows_buf[:, h, :] = att * (d_in[h] - delta[:, h : h + 1])
        rows_buf[:, PAD + h, :] = att
    acc = w_out[...]
    for r in range(block):
        a = rows_buf[r].astype(BF16)
        lhs = jnp.concatenate([a, a[:PAD]], 0)
        rhs = jnp.concatenate([w_hi, gpair[r], w_lo], 0)
        pg_out[r] = dot(lhs, rhs, TN).astype(BF16)
        acc = acc + dot(a[:PAD], pair[r], NN)
    w_out[...] = acc


def push_kernel(axes, sizes, total, x, out, slots, send, recv):
    count = math.prod(sizes)
    place = 0
    for axis, size in zip(axes, sizes):
        place = place * size + lax.axis_index(axis)
    copies = []
    for step in range(1, count):
        peer = lax.rem(place + step, count)
        device = {}
        rest = peer
        for axis, size in reversed(list(zip(axes, sizes))):
            device[axis] = lax.rem(rest, size)
            rest = rest // size
        copy = pltpu.make_async_remote_copy(
            src_ref=x,
            dst_ref=slots.at[place],
            send_sem=send.at[step],
            recv_sem=recv.at[place],
            device_id=device,
            device_id_type=pl.DeviceIdType.MESH,
        )
        copy.start()
        copies.append(copy)
    slots[place] = x[...]
    for step in range(1, count):
        source = lax.rem(place + step, count)
        pltpu.make_async_remote_copy(
            src_ref=x,
            dst_ref=slots.at[source],
            send_sem=send.at[step],
            recv_sem=recv.at[source],
            device_id=device,
            device_id_type=pl.DeviceIdType.MESH,
        ).wait_recv()
    for copy in copies:
        copy.wait_send()
    if total:
        acc = slots[0]
        for c in range(1, count):
            acc = acc + slots[c]
        out[...] = acc
    else:
        out[...] = slots[...]


def pushed(x, axes, total):
    sizes = tuple(lax.axis_size(axis) for axis in axes)
    count = math.prod(sizes)
    return pl.pallas_call(
        functools.partial(push_kernel, axes, sizes, total),
        in_specs=[pl.BlockSpec(memory_space=pltpu.VMEM)],
        out_specs=pl.BlockSpec(memory_space=pltpu.VMEM),
        out_shape=jax.ShapeDtypeStruct(x.shape if total else (count, *x.shape), F32),
        scratch_shapes=[
            pltpu.VMEM((count, *x.shape), F32),
            pltpu.SemaphoreType.DMA((count,)),
            pltpu.SemaphoreType.DMA((count,)),
        ],
        compiler_params=pltpu.CompilerParams(has_side_effects=True),
    )(x)


def turn(rotation, local):
    return jnp.sum(rotation[:, :, None, :] * local[None], axis=1)


def turn_back(rotation, vector):
    return jnp.sum(rotation[:, :, None, :] * vector[:, None], axis=0)


def frame_terms(grad_global, local):
    rotation_part = jnp.sum(grad_global[:, None] * local[None], axis=2)
    return jnp.concatenate([rotation_part, jnp.sum(grad_global, axis=1)[:, None, :]], axis=1)


def by_head(x, heads):
    points = x.shape[1] // heads
    return x.reshape(3, heads, points, -1).transpose(1, 0, 2, 3).reshape(heads, 3 * points, -1)


def by_axis(x):
    heads, rows, m = x.shape
    return x.reshape(heads, 3, rows // 3, m).transpose(1, 0, 2, 3).reshape(3, heads * rows // 3, m)


def pad_rows(x, rows):
    return jnp.pad(x, ((0, 0), (0, rows - x.shape[1]), (0, 0)))


def per_device(
    pair_rep, bias_weight, head_weight, queries, key_vectors, values, query_points, key_points,
    value_points, rotations, translations, residue_count, grad_output, grad_points, grad_pair,
):
    channels, heads = bias_weight.shape
    width = queries.shape[0] // heads
    qpoints = query_points.shape[1] // heads
    vpoints = value_points.shape[1] // heads
    n_rows = queries.shape[1]
    n_cols = key_vectors.shape[1]
    logit_scale = math.sqrt(1.0 / 3.0)
    point_scale = math.sqrt(2.0 / (9.0 * qpoints))
    inner_scale = 1.0 / math.sqrt(width)
    coef = 0.5 * logit_scale * point_scale * jax.nn.softplus(head_weight)
    row_start = lax.axis_index("row") * n_rows
    col_start = lax.axis_index("col") * n_cols
    rot_rows = lax.dynamic_slice_in_dim(rotations, row_start, n_rows, 2)
    shift_rows = lax.dynamic_slice_in_dim(translations, row_start, n_rows, 1)
    rot_cols = lax.dynamic_slice_in_dim(rotations, col_start, n_cols, 2)
    shift_cols = lax.dynamic_slice_in_dim(translations, col_start, n_cols, 1)
    qg = by_head(turn(rot_rows, query_points) + shift_rows[:, None, :], heads)
    kg = by_head(turn(rot_cols, key_points) + shift_cols[:, None, :], heads)
    vg = by_head(turn(rot_cols, value_points) + shift_cols[:, None, :], heads)
    grad_flat = turn(rot_rows, grad_points)
    gg = by_head(grad_flat, heads)
    q = queries.reshape(heads, width, n_rows)
    k = key_vectors.reshape(heads, width, n_cols)
    qsize = width + 3 * qpoints
    nq = -(-(qsize + 2) // 16) * 16
    nv = width + 3 * vpoints
    nvp = -(-nv // 16) * 16
    c3 = coef[:, None, None]
    q_square = jnp.sum(qg * qg, axis=1, keepdims=True)
    k_square = jnp.sum(kg * kg, axis=1, keepdims=True)
    qcat = pad_rows(
        jnp.concatenate(
            [
                logit_scale * inner_scale * q,
                2.0 * c3 * qg,
                jnp.broadcast_to(-c3, (heads, 1, n_rows)),
                -c3 * q_square,
            ],
            axis=1,
        ),
        nq,
    )
    kcat = pad_rows(
        jnp.concatenate([k, kg, k_square, jnp.ones((heads, 1, n_cols), F32)], axis=1), nq
    )
    gcat = pad_rows(
        jnp.concatenate([grad_output.reshape(heads, width, n_rows), gg], axis=1), nvp
    )
    vcat = pad_rows(jnp.concatenate([values.reshape(heads, width, n_cols), vg], axis=1), nvp)
    w_t = jnp.pad(bias_weight.T, ((0, PAD - heads), (0, 0)))
    scaled = logit_scale * w_t.astype(F32)
    gpair = pad_rows(grad_pair, PAD)
    limit = residue_count - col_start

    block = 8
    grid = (n_rows // block,)
    whole = lambda *shape: pl.BlockSpec(shape, lambda i: (0,) * len(shape))
    pair_spec = pl.BlockSpec((block, n_cols, channels), lambda i: (i, 0, 0))
    gpair_spec = pl.BlockSpec((block, PAD, channels), lambda i: (i, 0, 0))
    hij_spec = pl.BlockSpec((heads, block, n_cols), lambda i: (0, i, 0))
    stat_spec = pl.BlockSpec((block, 128), lambda i: (i, 0))
    cat_specs = [
        whole(heads, nq, n_rows),
        whole(heads, nq, n_cols),
        whole(heads, nvp, n_rows),
        whole(heads, nvp, n_cols),
    ]
    params = pltpu.CompilerParams(
        dimension_semantics=("arbitrary",), vmem_limit_bytes=VMEM_LIMIT
    )
    hij = jax.ShapeDtypeStruct((heads, n_rows, n_cols), F32)
    e_all, d_all, own = pl.pallas_call(
        functools.partial(forward_kernel, heads, block, logit_scale),
        grid=grid,
        in_specs=[
            pl.BlockSpec(memory_space=pltpu.SMEM),
            pair_spec,
            whole(PAD, channels),
            gpair_spec,
            *cat_specs,
        ],
        out_specs=[hij_spec, hij_spec, stat_spec],
        out_shape=[hij, hij, jax.ShapeDtypeStruct((n_rows, 128), F32)],
        scratch_shapes=[
            pltpu.VMEM((heads, n_rows, n_cols), F32),
            pltpu.VMEM((heads, n_rows, n_cols), F32),
            pltpu.VMEM((block, 2 * PAD, n_cols), F32),
        ],
        compiler_params=params,
    )(limit, pair_rep, w_t, gpair, qcat, kcat, gcat, vcat)

    stats = pushed(own, ("col",), False)
    peers = stats.shape[0]
    nk = nq + nv
    nr = nq + nv - width
    per_head = lambda *shape: pl.BlockSpec((1, *shape), lambda i: (i, 0, 0))
    key_out, query_out = pl.pallas_call(
        functools.partial(sums_kernel, nq, nv, width),
        grid=(heads,),
        in_specs=[
            per_head(n_rows, n_cols),
            per_head(n_rows, n_cols),
            whole(peers, n_rows, 128),
            whole(n_rows, 128),
            per_head(nq, n_rows),
            per_head(nq, n_cols),
            per_head(nvp, n_rows),
            per_head(nvp, n_cols),
        ],
        out_specs=[per_head(nk, n_cols), per_head(nr, n_rows)],
        out_shape=[
            jax.ShapeDtypeStruct((heads, nk, n_cols), F32),
            jax.ShapeDtypeStruct((heads, nr, n_rows), F32),
        ],
        compiler_params=params,
    )(e_all, d_all, stats, own, qcat, kcat, gcat, vcat)
    key_sum = lax.psum_scatter(
        key_out.reshape(heads * nk, n_cols), "row", scatter_dimension=1, tiled=True
    ).reshape(heads, nk, -1)
    query_sum = lax.psum_scatter(
        query_out.reshape(heads * nr, n_rows), "col", scatter_dimension=1, tiled=True
    ).reshape(heads, nr, -1)
    pair_grad, w_out = pl.pallas_call(
        functools.partial(pair_kernel, heads, block),
        grid=grid,
        in_specs=[
            pair_spec,
            hij_spec,
            hij_spec,
            pl.BlockSpec((peers, block, 128), lambda i: (0, i, 0)),
            stat_spec,
            whole(PAD, channels),
            gpair_spec,
        ],
        out_specs=[pair_spec, whole(PAD, channels)],
        out_shape=[
            jax.ShapeDtypeStruct(pair_rep.shape, BF16),
            jax.ShapeDtypeStruct((PAD, channels), F32),
        ],
        scratch_shapes=[pltpu.VMEM((block, 2 * PAD, n_cols), F32)],
        compiler_params=params,
        cost_estimate=pl.CostEstimate(
            flops=8 * n_rows * n_cols * channels * PAD,
            bytes_accessed=4 * n_rows * n_cols * channels + 8 * heads * n_rows * n_cols,
            transcendentals=0,
        ),
    )(pair_rep, e_all, d_all, stats, own, scaled, gpair)

    distance_part = jnp.sum(
        q_square[:, 0] * query_out[:, qsize + 1] + query_out[:, qsize], axis=1
    ) - 2.0 * jnp.sum(qg * query_out[:, width:qsize], axis=(1, 2))
    small = jnp.concatenate(
        [logit_scale * w_out, jnp.pad(distance_part, (0, 8 * channels - heads)).reshape(8, channels)]
    )
    small = pushed(small, ("row", "col"), True)
    weight_total = small[:heads].T
    head_weight_grad = (
        small[PAD, :heads] * (-0.5 * logit_scale * point_scale) * jax.nn.sigmoid(head_weight)
    )

    share = query_sum.shape[2]
    start = lax.axis_index("col") * share
    own_rows = lambda x: lax.dynamic_slice_in_dim(x, start, share, x.ndim - 1)
    rot_own = own_rows(rot_rows)
    shift_own = own_rows(shift_rows)
    query_grad = (logit_scale * inner_scale * query_sum[:, :width]).reshape(heads * width, share)
    dqg = by_axis(
        -2.0 * c3 * (own_rows(qg) * query_sum[:, qsize + 1][:, None] - query_sum[:, width:qsize])
    )
    point_out = by_axis(query_sum[:, nq:])
    query_point_grad = turn_back(rot_own, dqg)
    cotan_own = own_rows(grad_points)
    out_part = jnp.sum((point_out - shift_own[:, None, :])[:, None] * cotan_own[None], axis=2)
    out_part = jnp.concatenate(
        [out_part, -jnp.sum(own_rows(grad_flat), axis=1)[:, None, :]], axis=1
    )
    query_frame_grad = frame_terms(dqg, own_rows(query_points)) + out_part

    kshare = key_sum.shape[2]
    kstart = lax.axis_index("row") * kshare
    own_cols = lambda x: lax.dynamic_slice_in_dim(x, kstart, kshare, x.ndim - 1)
    rot_keys = own_cols(rot_cols)
    key_grad = key_sum[:, :width].reshape(heads * width, kshare)
    value_grad = key_sum[:, nq : nq + width].reshape(heads * width, kshare)
    dkg = by_axis(
        key_sum[:, width:qsize] + 2.0 * own_cols(kg) * key_sum[:, qsize][:, None]
    )
    dvg = by_axis(key_sum[:, nq + width :])
    key_point_grad = turn_back(rot_keys, dkg)
    value_point_grad = turn_back(rot_keys, dvg)
    key_frame_grad = frame_terms(dkg, own_cols(key_points)) + frame_terms(
        dvg, own_cols(value_points)
    )
    return (
        pair_grad, query_grad, query_point_grad, query_frame_grad, key_grad, value_grad,
        key_point_grad, value_point_grad, key_frame_grad, weight_total, head_weight_grad,
    )


def solution(mesh):
    return jax.shard_map(
        per_device,
        mesh=mesh,
        in_specs=(
            P("row", "col", None),
            P(),
            P(),
            P(None, "row"),
            P(None, "col"),
            P(None, "col"),
            P(None, None, "row"),
            P(None, None, "col"),
            P(None, None, "col"),
            P(),
            P(),
            P(),
            P(None, "row"),
            P(None, None, "row"),
            P("row", None, None),
        ),
        out_specs=(
            P("row", "col", None),
            P(None, ("row", "col")),
            P(None, None, ("row", "col")),
            P(None, None, ("row", "col")),
            P(None, ("col", "row")),
            P(None, ("col", "row")),
            P(None, None, ("col", "row")),
            P(None, None, ("col", "row")),
            P(None, None, ("col", "row")),
            P(),
            P(),
        ),
        check_vma=False,
    )
```

profile of v0, /device:TPU:0, one launch (start us, length us, event | category | flops | bytes accessed | tf_op | source)
XLA Modules:
  0.0 193.0 jit_solution(15438477673631403946)
XLA Ops:
  7.3 0.7 copy-done
  7.9 0.7 constant_dynamic-slice_fusion.10
  8.6 0.8 constant_dynamic-slice_fusion.8
  10.1 1.2 broadcast_multiply_fusion.3
  11.3 0.5 broadcast_multiply_fusion.4
  11.8 0.9 multiply_reduce_fusion.11
  12.8 1.6 broadcast_multiply_fusion.1
  14.4 1.0 multiply_reduce_fusion.3
  15.4 0.7 copy_bitcast_fusion.1
  16.1 0.3 copy.68
  16.3 0.6 pad.28.bias_w
  16.9 0.9 pad.29.gpair
  18.2 0.3 multiply_reduce_fusion.2
  18.5 0.2 reshape.167
  18.8 1.0 copy-done.2
  19.7 0.3 multiply_reduce_fusion
  20.4 0.3 copy-done.14
  21.0 0.7 select_maximum_fusion.1.gcat
  21.7 1.7 select_maximum_fusion.vcat
  23.4 0.3 maximum_maximum_fusion
  23.7 1.3 pad.31.kcat
  25.0 0.7 select_maximum_fusion.2.qcat
  25.7 31.1 %shard_map.230 = (f32[12,128,1024]{2,1,0:T(8,128)}, f32[12,128,1024]{2,1,0:T(8,128)}, f32[128,128]{1,0:T(8,128)}) custom-call(s32[1]{0:T(128)S(6)} %sub.25.limit_ref, bf16[128,1024,128]{2,1,0:T(8,128)(2,1)} %pair.3, bf16[16,128]{1,0:T(8,128)(2,1)} %pad.28.bias_w, bf16[128,16,128]{2,1,0:T(8,128)(2,1)} %pad.29.gpair, ...), custom_call_target="tpu_custom_call" | custom-call | tf_op jit(solution)/shard_map/pallas_call | solution.py:313
  56.8 13.0 %shard_map.231.stats = f32[2,128,128]{2,1,0:T(8,128)} custom-call(f32[128,128]{1,0:T(8,128)} %get-tuple-element.20.x.own), custom_call_target="tpu_custom_call" | custom-call | tf_op jit(solution)/shard_map/pallas_call | solution.py:197
  69.8 15.5 %shard_map.233 = (f32[12,72,1024]{2,1,0:T(8,128)}, f32[12,56,128]{2,1,0:T(8,128)}) custom-call(f32[12,128,1024]{2,1,0:T(8,128)} %get-tuple-element.18.e_in, f32[12,128,1024]{2,1,0:T(8,128)} %get-tuple-element.19.d_in, f32[2,128,128]{2,1,0:T(8,128)} %shard_map.231.stats, f32[128,128]{1,0:T(8,128)} %get-tuple-element.20.x.own, ...), custom_call_target="tpu_custom_call" | custom-call | tf_op jit(solution)/shard_map/pallas_call | solution.py:338
  85.3 1.9 copy.90
  87.3 5.0 %copy.92 = f32[864,1024]{0,1:T(8,128)} copy(f32[864,1024]{1,0:T(8,128)} %bitcast.96) | data formatting | bytes 7077888
  92.3 0.9 copy-done.1
  93.3 0.8 copy.85
  94.6 0.8 fusion.3
  95.6 0.6 convert_multiply_fusion.scaled
  96.2 38.6 %shard_map.232 = (bf16[128,1024,128]{2,1,0:T(8,128)(2,1)}, f32[16,128]{1,0:T(8,128)}) custom-call(bf16[128,1024,128]{2,1,0:T(8,128)(2,1)} %pair.3, f32[12,128,1024]{2,1,0:T(8,128)} %get-tuple-element.18.e_in, f32[12,128,1024]{2,1,0:T(8,128)} %get-tuple-element.19.d_in, f32[2,128,128]{2,1,0:T(8,128)} %shard_map.231.stats, ...), custom_call_target="tpu_custom_call" | custom-call | flops 2147483648 | bytes 79691776 | tf_op jit(solution)/shard_map/pallas_call | solution.py:364
  134.9 0.7 broadcast_multiply_fusion.2
  135.6 0.6 pad_maximum_fusion.x
  136.2 19.0 %shard_map.234 = f32[24,128]{1,0:T(8,128)} custom-call(f32[24,128]{1,0:T(8,128)} %pad_maximum_fusion.x), custom_call_target="tpu_custom_call" | custom-call | tf_op jit(solution)/shard_map/pallas_call | solution.py:197
  155.3 0.9 constant_dynamic-slice_fusion.2
  156.3 1.2 divide_multiply_fusion
  157.5 1.3 slice_bitcast_fusion.4
  158.8 1.1 copy.91
  160.3 0.7 copy.87
  161.2 19.2 %reduce-scatter.9.cloned.1.call-done = f32[64,864]{1,0:T(8,128)} async-done(((f32[1024,864]{1,0:T(8,128)}), f32[64,864]{1,0:T(8,128)}) %reduce-scatter.9.cloned.1.call-update) | async-done | bytes 221200
  180.4 1.1 copy.93
  182.0 0.7 copy.89
  182.7 0.7 copy.88
  183.4 0.8 multiply_reduce_fusion.4
  184.2 0.8 multiply_reduce_fusion.7
  185.0 0.6 maximum_add_fusion.1
  185.6 0.6 maximum_add_fusion
  (82 shorter events, 3.1 us)
Async XLA Ops:
  7.2 0.8 copy-start
  7.2 8.9 %copy-start.8 = (bf16[128,12,128]{2,0,1:T(8,128)(2,1)S(1)}, bf16[128,12,128]{2,0,1:T(8,128)(2,1)}, u32[]{:S(2)}) copy-start(bf16[128,12,128]{2,0,1:T(8,128)(2,1)} %param.29) | copy-start | bytes 1179652
  7.2 9.1 %copy-start.12 = (bf16[128,12]{0,1:T(8,128)(2,1)S(1)}, bf16[128,12]{0,1:T(8,128)(2,1)}, u32[]{:S(2)}) copy-start(bf16[128,12]{0,1:T(8,128)(2,1)} %param.16) | copy-start | bytes 9220
  7.2 151.6 %reduce-scatter.7.cloned.1.call-start = ((), (), s32[]{:S(2)}) async-start(), calls=%async_computation.2 | async-start | bytes 589824
  12.8 5.1 %copy-start.5 = (f32[3,48,1024]{2,1,0:T(8,128)S(1)}, f32[3,48,1024]{2,1,0:T(8,128)}, u32[]{:S(2)}) copy-start(f32[3,48,1024]{2,1,0:T(8,128)} %param.22) | copy-start | bytes 1769476
  18.4 1.3 copy-start.2
  20.0 0.7 copy-start.14
  20.0 0.9 copy-start.7
  20.0 1.0 copy-start.11
  20.0 1.7 copy-start.4
  21.7 1.7 copy-start.3
  23.7 1.4 copy-start.9
  87.3 93.2 %reduce-scatter.9.cloned.1.call-start = ((), (), s32[]{:S(2)}) async-start(), calls=%async_computation.3 | async-start | bytes 3899392
  92.3 1.0 copy-start.1
  92.3 1.8 copy-start.6
  96.2 59.9 %copy-start.10 = (f32[3,48,128]{2,1,0:T(8,128)S(1)}, f32[3,48,128]{2,1,0:T(8,128)}, u32[]{:S(2)}) copy-start(f32[3,48,128]{2,1,0:T(8,128)} %param.21) | copy-start | bytes 221188
  96.2 60.1 %copy-start.15 = (f32[12]{0:T(128)S(1)}, f32[12]{0:T(128)}, u32[]{:S(2)}) copy-start(f32[12]{0:T(128)} %param.17) | copy-start | bytes 148
  96.2 63.7 %copy-start.13 = (f32[12]{0:T(128)S(1)}, f32[12]{0:T(128)}, u32[]{:S(2)}) copy-start(f32[12]{0:T(128)} %get-tuple-element.75) | copy-start | bytes 148
Sparse Core Ops, SparseCore 0:
  87.4 13.2 reduce-scatter.6
  104.5 75.8 reduce-scatter.8
where the time goes:
time: 195 us; the launch traced here: 193 us
  Pallas kernels  117 us (60%)
  local copies, waits for them, and re-layouts  24.1 us (12%)
  waiting for transfers between devices  19.3 us (10%)
  other arithmetic  17.1 us (9%)
  between operations  15.2 us (8%)
    pallas_call x1, Pallas kernels, per_device(): pl.pallas_call(functools.partial(pair_kernel, heads, block), grid=grid, i...  38.6 us
    pallas_call x2, Pallas kernels, pushed(): pl.pallas_call(functools.partial(push_kernel, axes, sizes, total), in_spe...  32 us
    pallas_call x1, Pallas kernels, per_device(): pl.pallas_call(functools.partial(forward_kernel, heads, block, logit_scal...  31.1 us
    unnamed x4, waiting for transfers between devices  19.3 us
    pallas_call x1, Pallas kernels, per_device(): pl.pallas_call(functools.partial(sums_kernel, nq, nv, width), grid=(heads...  15.5 us
    unnamed x42, local copies, waits for them, and re-layouts  14.7 us
  transfers between devices with their start and end apart: 2, of which 1 were waited for; matrix products, arithmetic and copies ran while one was open for 8% of the time, Pallas kernels for 30%

commit v1 on v0

v1 whole, which is shorter than its diff:
```python
import functools
import math

import jax
import jax.numpy as jnp
from jax import lax
from jax.experimental import pallas as pl
from jax.experimental.pallas import tpu as pltpu
from jax.sharding import PartitionSpec as P

F32 = jnp.float32
BF16 = jnp.bfloat16
PAD = 16
VMEM_LIMIT = 67043328


def dot(a, b, dims):
    return lax.dot_general(a, b, (dims, ((), ())), preferred_element_type=F32)


TN = ((0,), (0,))
NT = ((1,), (1,))
NN = ((1,), (0,))


def split2(x):
    hi = x.astype(BF16)
    return hi, (x - hi.astype(F32)).astype(BF16)


def split3(x):
    hi = x.astype(BF16)
    rest = x - hi.astype(F32)
    mid = rest.astype(BF16)
    return hi, mid, (rest - mid.astype(F32)).astype(BF16)


def merged(stats, own):
    peers = stats.shape[0]
    top = stats[0]
    for c in range(1, peers):
        top = jnp.maximum(top, stats[c])
    total = jnp.zeros_like(top)
    upper = jnp.zeros_like(top)
    for c in range(peers):
        f = jnp.exp(stats[c] - top)
        total = total + pltpu.roll(stats[c], 128 - PAD, 1) * f
        upper = upper + pltpu.roll(stats[c], 128 - 2 * PAD, 1) * f
    return jnp.exp(own - top) / total, upper / total


def flip(place, bit):
    size = 1 << bit
    return place + size * (1 - 2 * ((place // size) % 2))


def toggled(place, bits):
    for bit in bits:
        place = flip(place, bit)
    return place


def subsets(bits):
    found = [()]
    for bit in bits:
        found = found + [s + (bit,) for s in found]
    return found


def remote(src, dst, send, recv, device):
    return pltpu.make_async_remote_copy(
        src_ref=src,
        dst_ref=dst,
        send_sem=send,
        recv_sem=recv,
        device_id=device,
        device_id_type=pl.DeviceIdType.MESH,
    )


class Scatter:
    def __init__(self, me, data, lanes, order, slots, send, recv):
        self.me, self.data, self.lanes, self.order = me, data, lanes, order
        self.slots, self.send, self.recv = slots, send, recv
        self.sent = []

    def plan(self, phase):
        first = sum(1 << (len(self.order) - 1 - p) for p in range(phase))
        return self.order[phase], list(enumerate(subsets(self.order[phase + 1 :]), first))

    def block(self, owner):
        return self.data.at[owner, :, self.lanes]

    def copy(self, phase, slot, bits):
        bit = self.order[phase]
        peer = flip(self.me, bit)
        return remote(
            self.block(toggled(peer, bits)),
            self.slots.at[slot],
            self.send.at[slot],
            self.recv.at[slot],
            {"row": peer},
        )

    def start(self, phase):
        _, blocks = self.plan(phase)
        for slot, bits in blocks:
            copy = self.copy(phase, slot, bits)
            copy.start()
            self.sent.append(copy)

    def finish(self, phase):
        _, blocks = self.plan(phase)
        for slot, bits in blocks:
            self.copy(phase, slot, bits).wait_recv()
            owner = toggled(self.me, bits)
            self.data[owner, :, self.lanes] = (
                self.data[owner, :, self.lanes] + self.slots[slot]
            )

    def drain(self):
        for copy in self.sent:
            copy.wait_send()


def main_kernel(
    shape, limit_ref, pair, bias_w, gpair, qcat, kcat, gcat, vcat, qraw,
    a_out, key_out, query_out, small_out,
    pair_buf, lbase, dbase, rows_buf, stats, merge_buf, key_rows, key_t, slots_a, slots_b,
    query_rows, query_t, qslots, small, small_col, small_row, a_stage,
    pair_sem, a_sem, stat_send, stat_recv, send_a, recv_a, send_b, recv_b, q_send, q_recv,
    col_send, col_recv, row_send, row_recv,
):
    heads, block, scale, nr_dev, nc_dev, nq, nv, vwidth, qsize = shape
    n_rows, cols = pair_buf.shape[0], pair_buf.shape[1]
    blocks = n_rows // block
    me = lax.axis_index("row")
    mc = lax.axis_index("col")
    row_peers = [lax.rem(me + s, nr_dev) for s in range(1, nr_dev)]
    col_peers = [lax.rem(mc + s, nc_dev) for s in range(1, nc_dev)]

    def load(i):
        rows = pl.ds(pl.multiple_of(i * block, block), block)
        return pltpu.make_async_copy(pair.at[rows], pair_buf.at[rows], pair_sem.at[i])

    def start_load(i, carry):
        load(i).start()
        return carry

    lax.fori_loop(0, blocks, start_load, 0)
    barrier = pltpu.get_barrier_semaphore()
    for peer in row_peers:
        pl.semaphore_signal(
            barrier, inc=1, device_id={"row": peer}, device_id_type=pl.DeviceIdType.MESH
        )
    for peer in col_peers:
        pl.semaphore_signal(
            barrier, inc=1, device_id={"col": peer}, device_id_type=pl.DeviceIdType.MESH
        )

    def base(h, carry):
        q0, q1, q2 = split3(qcat[h])
        k0, k1, k2 = split3(kcat[h])
        lbase[h] = dot(
            jnp.concatenate([q0, q0, q1, q0, q2, q1], 0),
            jnp.concatenate([k0, k1, k0, k2, k0, k1], 0),
            TN,
        )
        g0, g1 = split2(gcat[h])
        v0, v1 = split2(vcat[h])
        dbase[h] = dot(
            jnp.concatenate([g0, g0, g1], 0), jnp.concatenate([v0, v1, v0], 0), TN
        )
        return carry

    lax.fori_loop(0, heads, base, 0)
    valid = lax.broadcasted_iota(jnp.int32, (block, cols), 1) < limit_ref[0]
    lane = lax.broadcasted_iota(jnp.int32, (block, 128), 1)

    def forward(i, carry):
        load(i).wait()
        first = pl.multiple_of(i * block, block)
        rows = pl.ds(first, block)
        for r in range(block):
            w = jnp.concatenate([bias_w[...], gpair[first + r]], 0)
            rows_buf[r] = dot(w, pair_buf[first + r], NT)
        packed = jnp.ones((block, 128), F32)
        for h in range(heads):
            logit = lbase[h, rows, :] + scale * rows_buf[:, h, :]
            logit = jnp.where(valid, logit, F32(-1000000000.0))
            peak = jnp.max(logit, axis=1, keepdims=True)
            e = jnp.exp(logit - peak)
            d = dbase[h, rows, :] + rows_buf[:, PAD + h, :]
            lbase[h, rows, :] = e
            dbase[h, rows, :] = d
            packed = jnp.where(lane == h, peak, packed)
            packed = jnp.where(lane == PAD + h, jnp.sum(e, axis=1, keepdims=True), packed)
            packed = jnp.where(
                lane == 2 * PAD + h, jnp.sum(e * d, axis=1, keepdims=True), packed
            )
        stats[0, rows, :] = packed
        return carry

    lax.fori_loop(0, blocks, forward, 0)

    pl.semaphore_wait(barrier, nr_dev + nc_dev - 2)
    sent = []

    def stat_copy(s, peer):
        return remote(
            stats.at[0], stats.at[s], stat_send.at[s], stat_recv.at[s], {"col": peer}
        )

    for s, peer in enumerate(col_peers, 1):
        copy = stat_copy(s, peer)
        copy.start()
        sent.append(copy)
    for s, peer in enumerate(col_peers, 1):
        stat_copy(s, peer).wait_recv()
    factor, delta = merged(stats, stats[0])
    merge_buf[0] = factor
    merge_buf[1] = delta

    lane_of = lax.broadcasted_iota(jnp.int32, (n_rows, 128), 1)
    row_of = lax.broadcasted_iota(jnp.int32, (PAD, 128), 0)
    lane_small = lax.broadcasted_iota(jnp.int32, (PAD, 128), 1)
    small[...] = jnp.zeros_like(small)
    key_rows[...] = jnp.zeros_like(key_rows)
    query_rows[...] = jnp.zeros_like(query_rows)

    def sums(h, carry):
        mine = lane_of == h
        pick = lambda x: jnp.sum(jnp.where(mine, x, 0.0), axis=1, keepdims=True)
        att = lbase[h] * pick(merge_buf[0])
        dl = att * (dbase[h] - pick(merge_buf[1]))
        a0 = att.astype(BF16)
        d0, d1 = split2(dl)
        q = jnp.concatenate(split2(qcat[h]), 0)
        k = jnp.concatenate(split2(kcat[h]), 0)
        g = jnp.concatenate(split2(gcat[h]), 0)
        v = jnp.concatenate(split2(vcat[h]), 0)
        kk = dot(q, d0, NN) + dot(q, d1, NN)
        vv = dot(g, a0, NN)
        half = g.shape[0] // 2
        first = pl.multiple_of(h * (nq + nv), 8)
        key_rows[pl.ds(first, nq), :] = kk[:nq] + kk[nq:]
        key_rows[pl.ds(first + nq, nv), :] = vv[:nv] + vv[half : half + nv]
        qq = dot(k, d0, NT) + dot(k, d1, NT)
        qq = qq[:nq] + qq[nq:]
        oo = dot(v, a0, NT)
        first = pl.multiple_of(h * (nq + nv - vwidth), 8)
        query_rows[pl.ds(first, nq), :] = qq
        query_rows[pl.ds(first + nq, nv - vwidth), :] = (
            oo[vwidth:nv] + oo[half + vwidth : half + nv]
        )
        raw = qraw[h]
        span = qsize - vwidth
        part = raw[span : span + 1] * qq[qsize + 1 : qsize + 2] + qq[qsize : qsize + 1]
        part = part - 2.0 * jnp.sum(raw[:span] * qq[vwidth:qsize], axis=0, keepdims=True)
        part = jnp.sum(part, axis=1, keepdims=True)
        small[...] = small[...] + jnp.where(
            (row_of == heads) & (lane_small == h), part, 0.0
        )
        return carry

    lax.fori_loop(0, heads, sums, 0)

    share = cols // nr_dev
    for t in range(key_t.shape[2] // 128):
        part = slice(128 * t, 128 * t + 128)
        key_t[:, :, part] = key_rows[part, :].T.reshape(nr_dev, share, 128)
    qshare = n_rows // nc_dev
    for t in range(query_t.shape[2] // 128):
        part = slice(128 * t, 128 * t + 128)
        query_t[:, :, part] = query_rows[part, :].T.reshape(nc_dev, qshare, 128)

    bits = list(range(nr_dev.bit_length() - 1))
    swapped = bits[:1] + bits[1:3][::-1] + bits[3:]
    cut = slots_a.shape[2]
    streams = [
        Scatter(me, key_t, pl.ds(0, cut), bits, slots_a, send_a, recv_a),
        Scatter(me, key_t, pl.ds(cut, slots_b.shape[2]), swapped, slots_b, send_b, recv_b),
    ]

    def q_copy(s, peer):
        return remote(
            query_t.at[peer], qslots.at[s], q_send.at[s], q_recv.at[s], {"col": peer}
        )

    for s, peer in enumerate(col_peers):
        copy = q_copy(s, peer)
        copy.start()
        sent.append(copy)
    for stream in streams:
        stream.start(0)

    rows_buf[...] = jnp.zeros_like(rows_buf)

    def a_copy(i):
        rows = pl.ds(pl.multiple_of(i * block, block), block)
        slot = lax.rem(i, 2)
        return pltpu.make_async_copy(a_stage.at[slot], a_out.at[rows], a_sem.at[slot])

    def weights(i, carry):
        first = pl.multiple_of(i * block, block)
        rows = pl.ds(first, block)
        slot = lax.rem(i, 2)

        @pl.when(i >= 2)
        def _():
            a_copy(i - 2).wait()

        factor = merge_buf[0, rows, :]
        delta = merge_buf[1, rows, :]
        for h in range(heads):
            att = lbase[h, rows, :] * factor[:, h : h + 1]
            rows_buf[:, h, :] = att * (dbase[h, rows, :] - delta[:, h : h + 1])
            rows_buf[:, PAD + h, :] = att
        acc = small[...]
        for r in range(block):
            a = rows_buf[r].astype(BF16)
            a_stage[slot, r] = a
            acc = acc + scale * dot(a[:PAD], pair_buf[first + r], NN)
        small[...] = acc
        a_copy(i).start()
        return carry

    early = blocks // 4
    lax.fori_loop(0, early, weights, 0)
    for stream in streams:
        stream.finish(0)
        if len(bits) > 1:
            stream.start(1)
    lax.fori_loop(early, blocks, weights, 0)

    def col_copy(s, peer):
        return remote(
            small, small_col.at[s], col_send.at[s], col_recv.at[s], {"col": peer}
        )

    for s, peer in enumerate(col_peers):
        copy = col_copy(s, peer)
        copy.start()
        sent.append(copy)
    total = query_t[mc]
    for s, peer in enumerate(col_peers):
        q_copy(s, peer).wait_recv()
        total = total + qslots[s]
    query_out[...] = total

    for stream in streams:
        if len(bits) > 1:
            stream.finish(1)
        if len(bits) > 2:
            stream.start(2)

    total = small[...]
    for s, peer in enumerate(col_peers):
        col_copy(s, peer).wait_recv()
        total = total + small_col[s]
    small_row[0] = total

    def row_copy(s, peer):
        return remote(
            small_row.at[0], small_row.at[s], row_send.at[s], row_recv.at[s], {"row": peer}
        )

    for s, peer in enumerate(row_peers, 1):
        copy = row_copy(s, peer)
        copy.start()
        sent.append(copy)
    for phase in range(2, len(bits)):
        for stream in streams:
            stream.finish(phase)
            if phase + 1 < len(bits):
                stream.start(phase + 1)
    key_out[...] = key_t[me]
    total = small_row[0]
    for s, peer in enumerate(row_peers, 1):
        row_copy(s, peer).wait_recv()
        total = total + small_row[s]
    small_out[...] = total
    for copy in sent:
        copy.wait_send()
    for stream in streams:
        stream.drain()
    for i in range(max(blocks - 2, 0), blocks):
        a_copy(i).wait()


def pair_kernel(block, a_in, scaled, gpair, pg_out):
    w_hi, w_lo = split2(scaled[...])
    for r in range(block):
        a = a_in[r]
        lhs = jnp.concatenate([a, a[:PAD]], 0)
        rhs = jnp.concatenate([w_hi, gpair[r], w_lo], 0)
        pg_out[r] = dot(lhs, rhs, TN).astype(BF16)


def turn(rotation, local):
    return jnp.sum(rotation[:, :, None, :] * local[None], axis=1)


def turn_back(rotation, vector):
    return jnp.sum(rotation[:, :, None, :] * vector[:, None], axis=0)


def frame_terms(grad_global, local):
    rotation_part = jnp.sum(grad_global[:, None] * local[None], axis=2)
    return jnp.concatenate([rotation_part, jnp.sum(grad_global, axis=1)[:, None, :]], axis=1)


def by_head(x, heads):
    points = x.shape[1] // heads
    return x.reshape(3, heads, points, -1).transpose(1, 0, 2, 3).reshape(heads, 3 * points, -1)


def by_axis(x):
    heads, rows, m = x.shape
    return x.reshape(heads, 3, rows // 3, m).transpose(1, 0, 2, 3).reshape(3, heads * rows // 3, m)


def pad_rows(x, rows):
    return jnp.pad(x, ((0, 0), (0, rows - x.shape[1]), (0, 0)))


def per_device(
    pair_rep, bias_weight, head_weight, queries, key_vectors, values, query_points, key_points,
    value_points, rotations, translations, residue_count, grad_output, grad_points, grad_pair,
):
    channels, heads = bias_weight.shape
    width = queries.shape[0] // heads
    qpoints = query_points.shape[1] // heads
    vpoints = value_points.shape[1] // heads
    n_rows = queries.shape[1]
    n_cols = key_vectors.shape[1]
    logit_scale = math.sqrt(1.0 / 3.0)
    point_scale = math.sqrt(2.0 / (9.0 * qpoints))
    inner_scale = 1.0 / math.sqrt(width)
    coef = 0.5 * logit_scale * point_scale * jax.nn.softplus(head_weight)
    row_start = lax.axis_index("row") * n_rows
    col_start = lax.axis_index("col") * n_cols
    rot_rows = lax.dynamic_slice_in_dim(rotations, row_start, n_rows, 2)
    shift_rows = lax.dynamic_slice_in_dim(translations, row_start, n_rows, 1)
    rot_cols = lax.dynamic_slice_in_dim(rotations, col_start, n_cols, 2)
    shift_cols = lax.dynamic_slice_in_dim(translations, col_start, n_cols, 1)
    qg = by_head(turn(rot_rows, query_points) + shift_rows[:, None, :], heads)
    kg = by_head(turn(rot_cols, key_points) + shift_cols[:, None, :], heads)
    vg = by_head(turn(rot_cols, value_points) + shift_cols[:, None, :], heads)
    grad_flat = turn(rot_rows, grad_points)
    gg = by_head(grad_flat, heads)
    q = queries.reshape(heads, width, n_rows)
    k = key_vectors.reshape(heads, width, n_cols)
    qsize = width + 3 * qpoints
    nq = -(-(qsize + 2) // 16) * 16
    nv = width + 3 * vpoints
    nvp = -(-nv // 16) * 16
    c3 = coef[:, None, None]
    q_square = jnp.sum(qg * qg, axis=1, keepdims=True)
    k_square = jnp.sum(kg * kg, axis=1, keepdims=True)
    qcat = pad_rows(
        jnp.concatenate(
            [
                logit_scale * inner_scale * q,
                2.0 * c3 * qg,
                jnp.broadcast_to(-c3, (heads, 1, n_rows)),
                -c3 * q_square,
            ],
            axis=1,
        ),
        nq,
    )
    kcat = pad_rows(
        jnp.concatenate([k, kg, k_square, jnp.ones((heads, 1, n_cols), F32)], axis=1), nq
    )
    gcat = pad_rows(
        jnp.concatenate([grad_output.reshape(heads, width, n_rows), gg], axis=1), nvp
    )
    vcat = pad_rows(jnp.concatenate([values.reshape(heads, width, n_cols), vg], axis=1), nvp)
    w_t = jnp.pad(bias_weight.T, ((0, PAD - heads), (0, 0)))
    scaled = logit_scale * w_t.astype(F32)
    gpair = pad_rows(grad_pair, PAD)
    limit = residue_count - col_start

    block = 8
    rows_dev = lax.axis_size("row")
    cols_dev = lax.axis_size("col")
    qraw = pad_rows(jnp.concatenate([qg, q_square], axis=1), PAD)
    nk = nq + nv
    nr = nq + nv - width
    key_lanes = -(-heads * nk // 128) * 128
    query_lanes = -(-heads * nr // 128) * 128
    cut = -(-key_lanes // 256) * 128
    kshare = n_cols // rows_dev
    qshare = n_rows // cols_dev
    vmem = pl.BlockSpec(memory_space=pltpu.VMEM)
    anywhere = pl.BlockSpec(memory_space=pl.ANY)
    sems = lambda count: pltpu.SemaphoreType.DMA((max(count, 1),))
    a_all, key_part, query_part, small = pl.pallas_call(
        functools.partial(
            main_kernel,
            (heads, block, logit_scale, rows_dev, cols_dev, nq, nv, width, qsize),
        ),
        in_specs=[pl.BlockSpec(memory_space=pltpu.SMEM), anywhere] + [vmem] * 7,
        out_specs=[anywhere, vmem, vmem, vmem],
        out_shape=[
            jax.ShapeDtypeStruct((n_rows, 2 * PAD, n_cols), BF16),
            jax.ShapeDtypeStruct((kshare, key_lanes), F32),
            jax.ShapeDtypeStruct((qshare, query_lanes), F32),
            jax.ShapeDtypeStruct((PAD, channels), F32),
        ],
        scratch_shapes=[
            pltpu.VMEM((n_rows, n_cols, channels), BF16),
            pltpu.VMEM((heads, n_rows, n_cols), F32),
            pltpu.VMEM((heads, n_rows, n_cols), F32),
            pltpu.VMEM((block, 2 * PAD, n_cols), F32),
            pltpu.VMEM((cols_dev, n_rows, 128), F32),
            pltpu.VMEM((2, n_rows, 128), F32),
            pltpu.VMEM((key_lanes, n_cols), F32),
            pltpu.VMEM((rows_dev, kshare, key_lanes), F32),
            pltpu.VMEM((rows_dev - 1, kshare, cut), F32),
            pltpu.VMEM((rows_dev - 1, kshare, key_lanes - cut), F32),
            pltpu.VMEM((query_lanes, n_rows), F32),
            pltpu.VMEM((cols_dev, qshare, query_lanes), F32),
            pltpu.VMEM((max(cols_dev - 1, 1), qshare, query_lanes), F32),
            pltpu.VMEM((PAD, channels), F32),
            pltpu.VMEM((max(cols_dev - 1, 1), PAD, channels), F32),
            pltpu.VMEM((rows_dev, PAD, channels), F32),
            pltpu.VMEM((2, block, 2 * PAD, n_cols), BF16),
            sems(n_rows // block),
            sems(2),
            sems(cols_dev),
            sems(cols_dev),
            sems(rows_dev - 1),
            sems(rows_dev - 1),
            sems(rows_dev - 1),
            sems(rows_dev - 1),
            sems(cols_dev - 1),
            sems(cols_dev - 1),
            sems(cols_dev - 1),
            sems(cols_dev - 1),
            sems(rows_dev),
            sems(rows_dev),
        ],
        compiler_params=pltpu.CompilerParams(
            collective_id=0, has_side_effects=True, vmem_limit_bytes=VMEM_LIMIT
        ),
    )(limit, pair_rep, w_t, gpair, qcat, kcat, gcat, vcat, qraw)

    out_block = 8
    pair_grad = pl.pallas_call(
        functools.partial(pair_kernel, out_block),
        grid=(n_rows // out_block,),
        in_specs=[
            pl.BlockSpec((out_block, 2 * PAD, n_cols), lambda i: (i, 0, 0)),
            pl.BlockSpec((PAD, channels), lambda i: (0, 0)),
            pl.BlockSpec((out_block, PAD, channels), lambda i: (i, 0, 0)),
        ],
        out_specs=pl.BlockSpec((out_block, n_cols, channels), lambda i: (i, 0, 0)),
        out_shape=jax.ShapeDtypeStruct(pair_rep.shape, BF16),
        compiler_params=pltpu.CompilerParams(dimension_semantics=("arbitrary",)),
    )(a_all, scaled, gpair)

    key_sum = key_part.T[: heads * nk].reshape(heads, nk, kshare)
    query_sum = query_part.T[: heads * nr].reshape(heads, nr, qshare)
    weight_total = small[:heads].T
    head_weight_grad = (
        small[heads, :heads] * (-0.5 * logit_scale * point_scale) * jax.nn.sigmoid(head_weight)
    )

    share = query_sum.shape[2]
    start = lax.axis_index("col") * share
    own_rows = lambda x: lax.dynamic_slice_in_dim(x, start, share, x.ndim - 1)
    rot_own = own_rows(rot_rows)
    shift_own = own_rows(shift_rows)
    query_grad = (logit_scale * inner_scale * query_sum[:, :width]).reshape(heads * width, share)
    dqg = by_axis(
        -2.0 * c3 * (own_rows(qg) * query_sum[:, qsize + 1][:, None] - query_sum[:, width:qsize])
    )
    point_out = by_axis(query_sum[:, nq:])
    query_point_grad = turn_back(rot_own, dqg)
    cotan_own = own_rows(grad_points)
    out_part = jnp.sum((point_out - shift_own[:, None, :])[:, None] * cotan_own[None], axis=2)
    out_part = jnp.concatenate(
        [out_part, -jnp.sum(own_rows(grad_flat), axis=1)[:, None, :]], axis=1
    )
    query_frame_grad = frame_terms(dqg, own_rows(query_points)) + out_part

    kshare = key_sum.shape[2]
    kstart = lax.axis_index("row") * kshare
    own_cols = lambda x: lax.dynamic_slice_in_dim(x, kstart, kshare, x.ndim - 1)
    rot_keys = own_cols(rot_cols)
    key_grad = key_sum[:, :width].reshape(heads * width, kshare)
    value_grad = key_sum[:, nq : nq + width].reshape(heads * width, kshare)
    dkg = by_axis(
        key_sum[:, width:qsize] + 2.0 * own_cols(kg) * key_sum[:, qsize][:, None]
    )
    dvg = by_axis(key_sum[:, nq + width :])
    key_point_grad = turn_back(rot_keys, dkg)
    value_point_grad = turn_back(rot_keys, dvg)
    key_frame_grad = frame_terms(dkg, own_cols(key_points)) + frame_terms(
        dvg, own_cols(value_points)
    )
    return (
        pair_grad, query_grad, query_point_grad, query_frame_grad, key_grad, value_grad,
        key_point_grad, value_point_grad, key_frame_grad, weight_total, head_weight_grad,
    )


def solution(mesh):
    return jax.shard_map(
        per_device,
        mesh=mesh,
        in_specs=(
            P("row", "col", None),
            P(),
            P(),
            P(None, "row"),
            P(None, "col"),
            P(None, "col"),
            P(None, None, "row"),
            P(None, None, "col"),
            P(None, None, "col"),
            P(),
            P(),
            P(),
            P(None, "row"),
            P(None, None, "row"),
            P("row", None, None),
        ),
        out_specs=(
            P("row", "col", None),
            P(None, ("row", "col")),
            P(None, None, ("row", "col")),
            P(None, None, ("row", "col")),
            P(None, ("col", "row")),
            P(None, ("col", "row")),
            P(None, None, ("col", "row")),
            P(None, None, ("col", "row")),
            P(None, None, ("col", "row")),
            P(),
            P(),
        ),
        check_vma=False,
    )
```

time: 195 us -> 139 us (0.71)
  waiting for transfers between devices: 19.3 us -> 0 us
  Pallas kernels: 117 us -> 98.1 us
  between operations: 15.2 us -> 1.85 us
  local copies, waits for them, and re-layouts: 24.1 us -> 21.7 us
    unnamed x4 -> x0, waiting for transfers between devices: 19.3 us -> none
    pallas_call x5 -> x2, Pallas kernels: 117 us -> 98.1 us  [the longest x1 77.5 us: per_device(): pl.pallas_call(functools.partial(main_kernel, (heads, block, logit_scale,...]
    unnamed x42, local copies, waits for them, and re-layouts: 14.7 us -> 3.49 us
    dynamic_slice x3, local copies, waits for them, and re-layouts: 0.26 us -> 3.78 us  [per_device(): own_rows = lambda x: lax.dynamic_slice_in_dim(x, start, share, x.ndim - 1)]
    dynamic_slice x4, local copies, waits for them, and re-layouts: 1.16 us -> 3.91 us  [per_device(): own_cols = lambda x: lax.dynamic_slice_in_dim(x, kstart, kshare, x.ndim - 1)]
  transfers between devices with their start and end apart: 2 -> 0, of which waited for: 1 -> 0; matrix products, arithmetic and copies ran while one was open for 8% -> 0% of each run, Pallas kernels for 30% -> 0%
where the time goes in v1:
time: 139 us; the launch traced here: 137 us
  Pallas kernels  98.1 us (71%)
  local copies, waits for them, and re-layouts  21.7 us (16%)
  other arithmetic  15.6 us (11%)
  between operations  1.85 us (1%)
    pallas_call x1, Pallas kernels, per_device(): pl.pallas_call(functools.partial(main_kernel, (heads, block, logit_scale,...  77.5 us
    pallas_call x1, Pallas kernels, per_device(): pl.pallas_call(functools.partial(pair_kernel, out_block), grid=(n_rows //...  20.7 us
    dynamic_slice x4, local copies, waits for them, and re-layouts, per_device(): own_cols = lambda x: lax.dynamic_slice_in_dim(x, kstart, kshare, x.ndim - 1)  3.91 us
    dynamic_slice x3, local copies, waits for them, and re-layouts, per_device(): own_rows = lambda x: lax.dynamic_slice_in_dim(x, start, share, x.ndim - 1)  3.78 us
    unnamed x42, local copies, waits for them, and re-layouts  3.49 us

profile of v1, /device:TPU:0, one launch (start us, length us, event | category | flops | bytes accessed | tf_op | source)
XLA Modules:
  0.0 137.4 jit_solution(393057512451595373)
XLA Ops:
  1.5 1.2 broadcast_multiply_fusion.3
  2.7 0.7 constant_dynamic-slice_fusion.9
  3.3 1.3 constant_dynamic-slice_fusion.4
  4.7 1.3 pad.28.bias_w
  6.0 0.7 constant_dynamic-slice_fusion.10
  6.7 1.3 convert_multiply_fusion.scaled
  8.0 1.5 %constant_dynamic-slice_fusion.2 = (f32[3,3,64]{2,1,0:T(4,128)}, f32[3,3,64]{2,1,0:T(4,128)}) fusion(f32[3,3,2048]{2,1,0:T(4,128)} %param.24, s32[]{:T(128)S(6)} %dynamic_slice.60, s32[]{:T(128)S(6)} %dynamic_slice.53), kind=kLoop, calls=%fused_computation.53 | loop fusion | bytes 9224 | tf_op jit(solution)/shard_map/dynamic_slice | solution.py:591
  9.5 0.7 constant_dynamic-slice_fusion.7
  10.2 0.8 constant_dynamic-slice_fusion.8
  11.0 0.9 multiply_reduce_fusion.11
  12.1 1.7 %constant_dynamic-slice_fusion.5 = f32[3,48,64]{2,1,0:T(8,128)} fusion(f32[3,48,128]{2,1,0:T(8,128)} %param.21, s32[]{:T(128)S(6)} %select_n.37), kind=kLoop, calls=%fused_computation.56 | loop fusion | bytes 73732 | tf_op jit(solution)/shard_map/dynamic_slice | solution.py:573
  13.8 1.6 %constant_dynamic-slice_fusion.1 = f32[3,48,64]{2,1,0:T(8,128)} fusion(f32[3,48,1024]{2,1,0:T(8,128)} %param.22, s32[]{:T(128)S(6)} %select_n.40), kind=kLoop, calls=%fused_computation.52 | loop fusion | bytes 73732 | tf_op jit(solution)/shard_map/dynamic_slice | solution.py:591
  15.5 0.7 select_maximum_fusion.5.qraw
  16.2 0.7 select_maximum_fusion.2.qcat
  17.0 0.1 dynamic-slice_reduce_fusion
  17.1 0.6 copy.61
  17.7 0.7 copy.60
  18.5 0.7 select_maximum_fusion.1.gcat
  19.3 0.7 copy.67
  20.1 0.3 copy.50
  20.3 0.9 pad.29.gpair
  21.2 0.1 multiply_reduce_fusion.1
  21.4 0.2 reduce_sum.166
  21.6 0.3 multiply_reduce_fusion.2
  21.9 0.2 reshape.158
  22.2 0.3 multiply_reduce_fusion
  22.5 0.1 copy_bitcast_fusion
  22.6 1.0 copy-done.4
  23.6 1.7 %select_maximum_fusion.vcat = f32[12,48,1024]{2,1,0:T(8,128)} fusion(f32[12,24,1024]{2,1,0:T(8,128)S(1)} %copy_bitcast_fusion, f32[12,16,1024]{2,1,0:T(8,128)S(1)} %bitcast.89), kind=kLoop, calls=%fused_computation.1 | loop fusion | flops 2359296 | bytes 4325376 | tf_op jit(solution)/shard_map/concatenate | solution.py:479
  25.3 0.3 maximum_maximum_fusion
  25.6 1.3 pad.31.kcat
  26.9 77.5 %shard_map.230 = (bf16[128,32,1024]{2,1,0:T(8,128)(2,1)}, f32[64,896]{1,0:T(8,128)}, f32[64,768]{1,0:T(8,128)}, f32[16,128]{1,0:T(8,128)}) custom-call(s32[1]{0:T(128)S(6)} %sub.22.limit_ref, bf16[128,1024,128]{2,1,0:T(8,128)(2,1)} %pair.1, bf16[16,128]{1,0:T(8,128)(2,1)} %pad.28.bias_w, bf16[128,16,128]{2,1,0:T(8,128)(2,1)} %pad.29.gpair, ...), custom_call_target="tpu_custom_call" | custom-call | tf_op jit(solution)/shard_map/pallas_call | solution.py:499
  104.4 1.3 divide_multiply_fusion
  105.7 1.3 slice_bitcast_fusion.2
  107.0 1.1 copy.55
  108.1 1.0 fusion.1
  109.3 0.7 bitcast_subtract_fusion
  110.1 0.2 multiply_reduce_fusion.6
  110.3 0.7 copy.69
  111.0 0.2 copy.62
  111.2 1.0 slice_add_fusion
  112.4 0.8 multiply_reduce_fusion.7
  113.1 0.6 maximum_add_fusion
  113.9 0.8 multiply_reduce_fusion.4
  114.7 0.6 maximum_add_fusion.1
  115.3 0.7 copy.71
  116.0 0.7 copy.70
  116.7 20.7 %shard_map.231 = bf16[128,1024,128]{2,1,0:T(8,128)(2,1)} custom-call(bf16[128,32,1024]{2,1,0:T(8,128)(2,1)} %get-tuple-element.15.a_in, f32[16,128]{1,0:T(8,128)} %convert_multiply_fusion.scaled, bf16[128,16,128]{2,1,0:T(8,128)(2,1)} %pad.29.gpair), custom_call_target="tpu_custom_call" | custom-call | tf_op jit(solution)/shard_map/pallas_call | solution.py:551
  (70 shorter events, 1.2 us)
Async XLA Ops:
  0.6 16.3 %copy-start.6 = (f32[3,96,128]{2,1,0:T(8,128)S(1)}, f32[3,96,128]{2,1,0:T(8,128)}, u32[]{:S(2)}) copy-start(f32[3,96,128]{2,1,0:T(8,128)} %param.28) | copy-start | bytes 442372
  0.7 15.5 %copy-start.13 = (f32[192,128]{1,0:T(8,128)S(1)}, f32[192,128]{1,0:T(8,128)}, u32[]{:S(2)}) copy-start(f32[192,128]{1,0:T(8,128)} %param.18) | copy-start | bytes 294916
  11.9 6.5 %copy-start.14 = (f32[192,128]{1,0:T(8,128)S(1)}, f32[192,128]{1,0:T(8,128)}, u32[]{:S(2)}) copy-start(f32[192,128]{1,0:T(8,128)} %param.27) | copy-start | bytes 294916
  12.1 7.2 %copy-start.1 = (f32[12,12,128]{2,1,0:T(8,128)}, f32[12,12,128]{2,1,0:T(8,128)S(1)}, u32[]{:S(2)}) copy-start(f32[12,12,128]{2,1,0:T(8,128)S(1)} %reshape.156) | copy-start | bytes 221188
  12.1 7.1 %copy-start.2 = (f32[3,96,1024]{2,1,0:T(8,128)S(1)}, f32[3,96,1024]{2,1,0:T(8,128)}, u32[]{:S(2)}) copy-start(f32[3,96,1024]{2,1,0:T(8,128)} %param.23) | copy-start | bytes 3538948
  16.1 3.9 %copy-start.7 = (bf16[128,12,128]{2,0,1:T(8,128)(2,1)S(1)}, bf16[128,12,128]{2,0,1:T(8,128)(2,1)}, u32[]{:S(2)}) copy-start(bf16[128,12,128]{2,0,1:T(8,128)(2,1)} %param.29) | copy-start | bytes 1179652
  18.5 2.8 %copy-start.5 = (f32[3,48,1024]{2,1,0:T(8,128)S(1)}, f32[3,48,1024]{2,1,0:T(8,128)}, u32[]{:S(2)}) copy-start(f32[3,48,1024]{2,1,0:T(8,128)} %param.22) | copy-start | bytes 1769476
  22.2 3.1 %copy-start = (f32[12,12,1024]{2,1,0:T(8,128)}, f32[12,12,1024]{2,1,0:T(8,128)S(1)}, u32[]{:S(2)}) copy-start(f32[12,12,1024]{2,1,0:T(8,128)S(1)} %reshape.158) | copy-start | bytes 1769476
  22.4 1.1 copy-start.4
  23.6 1.7 %copy-start.3 = (f32[192,1024]{1,0:T(8,128)S(1)}, f32[192,1024]{1,0:T(8,128)}, u32[]{:S(2)}) copy-start(f32[192,1024]{1,0:T(8,128)} %param.19) | copy-start | bytes 2359300
  104.4 5.7 %copy-start.8 = (f32[3,96,64]{1,2,0:T(8,128)S(1)}, f32[3,96,64]{1,2,0:T(8,128)}, u32[]{:S(2)}) copy-start(f32[3,96,64]{1,2,0:T(8,128)} %copy.60) | copy-start | bytes 221188
  104.4 6.6 %copy-start.12 = (f32[64,896]{1,0:T(8,128)S(1)}, f32[64,896]{1,0:T(8,128)}, u32[]{:S(2)}) copy-start(f32[64,896]{1,0:T(8,128)} %get-tuple-element.17) | copy-start | bytes 688132
  109.1 3.2 %copy-start.10 = (f32[3,48,64]{2,1,0:T(8,128)S(1)}, f32[3,48,64]{2,1,0:T(8,128)}, u32[]{:S(2)}) copy-start(f32[3,48,64]{2,1,0:T(8,128)} %constant_dynamic-slice_fusion.5) | copy-start | bytes 110596
  109.1 3.2 %copy-start.11 = (f32[3,48,64]{2,1,0:T(8,128)S(1)}, f32[3,48,64]{2,1,0:T(8,128)}, u32[]{:S(2)}) copy-start(f32[3,48,64]{2,1,0:T(8,128)} %constant_dynamic-slice_fusion.1) | copy-start | bytes 110596
  109.1 3.2 %copy-start.15 = (f32[3,3,64]{2,1,0:T(4,128)S(1)}, f32[3,3,64]{2,1,0:T(4,128)}, u32[]{:S(2)}) copy-start(f32[3,3,64]{2,1,0:T(4,128)} %get-tuple-element.66) | copy-start | bytes 6916
  109.1 3.2 %copy-start.16 = (f32[3,3,64]{2,1,0:T(4,128)S(1)}, f32[3,3,64]{2,1,0:T(4,128)}, u32[]{:S(2)}) copy-start(f32[3,3,64]{2,1,0:T(4,128)} %get-tuple-element.67) | copy-start | bytes 6916
  109.2 3.9 %copy-start.17 = (f32[3,1,64]{2,1,0:T(1,128)S(1)}, f32[3,1,64]{2,1,0:T(1,128)}, u32[]{:S(2)}) copy-start(f32[3,1,64]{2,1,0:T(1,128)} %copy.61) | copy-start | bytes 2308
  110.2 3.6 %copy-start.9 = (f32[3,96,64]{1,2,0:T(8,128)S(1)}, f32[3,96,64]{1,2,0:T(8,128)}, u32[]{:S(2)}) copy-start(f32[3,96,64]{1,2,0:T(8,128)} %copy.67) | copy-start | bytes 221188

commit v2 on v1

--- a/solution.py
+++ b/solution.py
@@ -79,8 +79,8 @@
 
 
 class Scatter:
-    def __init__(self, me, data, lanes, order, slots, send, recv):
-        self.me, self.data, self.lanes, self.order = me, data, lanes, order
+    def __init__(self, me, data, part, order, slots, send, recv):
+        self.me, self.data, self.part, self.order = me, data, part, order
         self.slots, self.send, self.recv = slots, send, recv
         self.sent = []
 
@@ -89,7 +89,7 @@
         return self.order[phase], list(enumerate(subsets(self.order[phase + 1 :]), first))
 
     def block(self, owner):
-        return self.data.at[owner, :, self.lanes]
+        return self.data.at[(owner, *self.part)]
 
     def copy(self, phase, slot, bits):
         bit = self.order[phase]
@@ -114,30 +114,71 @@
         for slot, bits in blocks:
             self.copy(phase, slot, bits).wait_recv()
             owner = toggled(self.me, bits)
-            self.data[owner, :, self.lanes] = (
-                self.data[owner, :, self.lanes] + self.slots[slot]
-            )
+            place = (owner, *self.part)
+            self.data[place] = self.data[place] + self.slots[slot]
 
     def drain(self):
         for copy in self.sent:
             copy.wait_send()
 
 
+def filled(x, step):
+    rest = -x.shape[0] % step
+    return jnp.concatenate([x, jnp.zeros((rest, x.shape[1]), F32)], 0) if rest else x
+
+
+def window(start, size, total):
+    return slice(None) if total == size else pl.ds(pl.multiple_of(start, 128), size)
+
+
+def turned(rot, shift, local, lanes):
+    out = []
+    for x in range(3):
+        total = rot[x, 0:1, lanes] * local(0)
+        for y in range(1, 3):
+            total = total + rot[x, y : y + 1, lanes] * local(y)
+        if shift is not None:
+            total = total + shift[x : x + 1, lanes]
+        out.append(total)
+    return out
+
+
+def point_coef(head_w, factor):
+    x = head_w[...]
+    return factor * (jnp.maximum(x, 0.0) + jnp.log(1.0 + jnp.exp(-jnp.abs(x))))
+
+
+def pick_lane(row, lane):
+    mine = lax.broadcasted_iota(jnp.int32, row.shape, 1) == lane
+    return jnp.sum(jnp.where(mine, row, 0.0), axis=1, keepdims=True)
+
+
 def main_kernel(
-    shape, limit_ref, pair, bias_w, gpair, qcat, kcat, gcat, vcat, qraw,
-    a_out, key_out, query_out, small_out,
+    shape, limit_ref, pair, bias_in, gpair, head_w, queries, query_points, grad_output,
+    grad_points, rot_r, shift_r, rot_c, shift_c, key_in, value_in, key_points, value_points,
+    a_out, key_out, key_away, query_out, small_out,
     pair_buf, lbase, dbase, rows_buf, stats, merge_buf, key_rows, key_t, slots_a, slots_b,
-    query_rows, query_t, qslots, small, small_col, small_row, a_stage,
-    pair_sem, a_sem, stat_send, stat_recv, send_a, recv_a, send_b, recv_b, q_send, q_recv,
+    query_rows, query_t, qslots, small, small_col, small_row,
+    bias_w, qcat, kcat, gcat, vcat, qraw,
+    pair_sem, a_sem, in_sem, stat_send, stat_recv, send_a, recv_a, send_b, recv_b, q_send, q_recv,
     col_send, col_recv, row_send, row_recv,
 ):
-    heads, block, scale, nr_dev, nc_dev, nq, nv, vwidth, qsize = shape
+    heads, block, scale, inner, point_factor, nr_dev, nc_dev, nq, nv, vwidth, qsize = shape
     n_rows, cols = pair_buf.shape[0], pair_buf.shape[1]
     blocks = n_rows // block
     me = lax.axis_index("row")
     mc = lax.axis_index("col")
     row_peers = [lax.rem(me + s, nr_dev) for s in range(1, nr_dev)]
     col_peers = [lax.rem(mc + s, nc_dev) for s in range(1, nc_dev)]
+    nkp, nvp = key_points.shape[0], value_points.shape[0]
+    incoming = [
+        pltpu.make_async_copy(key_points, key_rows.at[pl.ds(nvp, nkp)], in_sem.at[0]),
+        pltpu.make_async_copy(value_points, key_rows.at[pl.ds(0, nvp)], in_sem.at[1]),
+        pltpu.make_async_copy(key_in, kcat.at[:, pl.ds(0, vwidth), :], in_sem.at[2]),
+        pltpu.make_async_copy(value_in, vcat.at[:, pl.ds(0, vwidth), :], in_sem.at[3]),
+    ]
+    for copy in incoming:
+        copy.start()
 
     def load(i):
         rows = pl.ds(pl.multiple_of(i * block, block), block)
@@ -157,6 +198,59 @@
         pl.semaphore_signal(
             barrier, inc=1, device_id={"col": peer}, device_id_type=pl.DeviceIdType.MESH
         )
+
+    channels = bias_in.shape[1]
+    bias_w[...] = jnp.concatenate(
+        [bias_in[...].astype(F32), jnp.zeros((PAD - heads, channels), F32)], 0
+    ).astype(BF16)
+    coef = point_coef(head_w, point_factor)
+    qpoints, vpoints = (qsize - vwidth) // 3, (nv - vwidth) // 3
+    span = qsize - vwidth
+    lanes = window(me * n_rows, n_rows, rot_r.shape[2])
+    qg = turned(rot_r, shift_r, lambda y: query_points[y], lanes)
+    gg = turned(rot_r, None, lambda y: grad_points[y], lanes)
+    q_square = qg[0] * qg[0] + qg[1] * qg[1] + qg[2] * qg[2]
+    for h in range(heads):
+        c = pick_lane(coef, h)
+        own = slice(vwidth * h, vwidth * h + vwidth)
+        points = slice(qpoints * h, qpoints * h + qpoints)
+        qcat[h, 0:vwidth] = (scale * inner) * queries[own]
+        gcat[h, 0:vwidth] = grad_output[own]
+        for x in range(3):
+            piece = qg[x][points]
+            qraw[h, qpoints * x : qpoints * x + qpoints] = piece
+            at = vwidth + qpoints * x
+            qcat[h, at : at + qpoints] = (2.0 * c) * piece
+            at = vwidth + vpoints * x
+            gcat[h, at : at + vpoints] = gg[x][vpoints * h : vpoints * h + vpoints]
+        square = jnp.sum(q_square[points], axis=0, keepdims=True)
+        qraw[h, span : span + 1] = square
+        qcat[h, qsize : qsize + 1] = jnp.broadcast_to(-c, (1, n_rows))
+        qcat[h, qsize + 1 : qsize + 2] = -c * square
+        qcat[h, qsize + 2 : nq] = jnp.zeros((nq - qsize - 2, n_rows), F32)
+
+    lanes = window(mc * cols, cols, rot_c.shape[2])
+    incoming[0].wait()
+    incoming[2].wait()
+    part = nkp // 3
+    kg = turned(rot_c, shift_c, lambda y: key_rows[nvp + part * y : nvp + part * y + part], lanes)
+    k_square = kg[0] * kg[0] + kg[1] * kg[1] + kg[2] * kg[2]
+    for h in range(heads):
+        points = slice(qpoints * h, qpoints * h + qpoints)
+        for x in range(3):
+            at = vwidth + qpoints * x
+            kcat[h, at : at + qpoints] = kg[x][points]
+        kcat[h, qsize : qsize + 1] = jnp.sum(k_square[points], axis=0, keepdims=True)
+        kcat[h, qsize + 1 : qsize + 2] = jnp.ones((1, cols), F32)
+        kcat[h, qsize + 2 : nq] = jnp.zeros((nq - qsize - 2, cols), F32)
+    incoming[1].wait()
+    incoming[3].wait()
+    part_v = nvp // 3
+    vg = turned(rot_c, shift_c, lambda y: key_rows[part_v * y : part_v * y + part_v], lanes)
+    for h in range(heads):
+        for x in range(3):
+            at = vwidth + vpoints * x
+            vcat[h, at : at + vpoints] = vg[x][vpoints * h : vpoints * h + vpoints]
 
     def base(h, carry):
         q0, q1, q2 = split3(qcat[h])
@@ -166,15 +260,16 @@
             jnp.concatenate([k0, k1, k0, k2, k0, k1], 0),
             TN,
         )
-        g0, g1 = split2(gcat[h])
-        v0, v1 = split2(vcat[h])
+        g0, g1 = split2(filled(gcat[h], PAD))
+        v0, v1 = split2(filled(vcat[h], PAD))
         dbase[h] = dot(
             jnp.concatenate([g0, g0, g1], 0), jnp.concatenate([v0, v1, v0], 0), TN
         )
         return carry
 
     lax.fori_loop(0, heads, base, 0)
-    valid = lax.broadcasted_iota(jnp.int32, (block, cols), 1) < limit_ref[0]
+    limit = limit_ref[0] - mc * cols
+    valid = lax.broadcasted_iota(jnp.int32, (block, cols), 1) < limit
     lane = lax.broadcasted_iota(jnp.int32, (block, 128), 1)
 
     def forward(i, carry):
@@ -237,8 +332,8 @@
         d0, d1 = split2(dl)
         q = jnp.concatenate(split2(qcat[h]), 0)
         k = jnp.concatenate(split2(kcat[h]), 0)
-        g = jnp.concatenate(split2(gcat[h]), 0)
-        v = jnp.concatenate(split2(vcat[h]), 0)
+        g = jnp.concatenate(split2(filled(gcat[h], PAD)), 0)
+        v = jnp.concatenate(split2(filled(vcat[h], PAD)), 0)
         kk = dot(q, d0, NN) + dot(q, d1, NN)
         vv = dot(g, a0, NN)
         half = g.shape[0] // 2
@@ -276,11 +371,18 @@
 
     bits = list(range(nr_dev.bit_length() - 1))
     swapped = bits[:1] + bits[1:3][::-1] + bits[3:]
-    cut = slots_a.shape[2]
+    lane_count = key_t.shape[2]
+    if slots_a.shape[2] == lane_count:
+        cut = slots_a.shape[1]
+        parts = [(pl.ds(0, cut), slice(None)), (pl.ds(cut, share - cut), slice(None))]
+    else:
+        cut = slots_a.shape[2]
+        parts = [(slice(None), pl.ds(0, cut)), (slice(None), pl.ds(cut, lane_count - cut))]
     streams = [
-        Scatter(me, key_t, pl.ds(0, cut), bits, slots_a, send_a, recv_a),
-        Scatter(me, key_t, pl.ds(cut, slots_b.shape[2]), swapped, slots_b, send_b, recv_b),
+        Scatter(me, key_t, parts[0], bits, slots_a, send_a, recv_a),
+        Scatter(me, key_t, parts[1], swapped, slots_b, send_b, recv_b),
     ]
+    last = len(bits) - 1
 
     def q_copy(s, peer):
         return remote(
@@ -292,24 +394,22 @@
         copy.start()
         sent.append(copy)
     for stream in streams:
-        stream.start(0)
+        if last > 0:
+            stream.start(0)
 
     rows_buf[...] = jnp.zeros_like(rows_buf)
+
+    depth = a_out.shape[1]
 
     def a_copy(i):
         rows = pl.ds(pl.multiple_of(i * block, block), block)
-        slot = lax.rem(i, 2)
-        return pltpu.make_async_copy(a_stage.at[slot], a_out.at[rows], a_sem.at[slot])
+        return pltpu.make_async_copy(
+            pair_buf.at[rows, pl.ds(0, depth), :], a_out.at[rows], a_sem.at[i]
+        )
 
     def weights(i, carry):
         first = pl.multiple_of(i * block, block)
         rows = pl.ds(first, block)
-        slot = lax.rem(i, 2)
-
-        @pl.when(i >= 2)
-        def _():
-            a_copy(i - 2).wait()
-
         factor = merge_buf[0, rows, :]
         delta = merge_buf[1, rows, :]
         for h in range(heads):
@@ -319,19 +419,28 @@
         acc = small[...]
         for r in range(block):
             a = rows_buf[r].astype(BF16)
-            a_stage[slot, r] = a
             acc = acc + scale * dot(a[:PAD], pair_buf[first + r], NN)
+            for c in range(cols // 128):
+                pair_buf[first + r, 2 * PAD * c : 2 * PAD * c + 2 * PAD, :] = a[
+                    :, 128 * c : 128 * c + 128
+                ]
         small[...] = acc
-        a_copy(i).start()
+
+        @pl.when(i > 0)
+        def _():
+            a_copy(i - 1).start()
+
         return carry
 
     early = blocks // 4
     lax.fori_loop(0, early, weights, 0)
     for stream in streams:
-        stream.finish(0)
-        if len(bits) > 1:
+        if last > 0:
+            stream.finish(0)
+        if last > 1:
             stream.start(1)
     lax.fori_loop(early, blocks, weights, 0)
+    a_copy(blocks - 1).start()
 
     def col_copy(s, peer):
         return remote(
@@ -346,12 +455,12 @@
     for s, peer in enumerate(col_peers):
         q_copy(s, peer).wait_recv()
         total = total + qslots[s]
-    query_out[...] = total
+    query_t[mc] = total
 
     for stream in streams:
-        if len(bits) > 1:
+        if last > 1:
             stream.finish(1)
-        if len(bits) > 2:
+        if last > 2:
             stream.start(2)
 
     total = small[...]
@@ -369,55 +478,194 @@
         copy = row_copy(s, peer)
         copy.start()
         sent.append(copy)
-    for phase in range(2, len(bits)):
+    for phase in range(2, last):
         for stream in streams:
             stream.finish(phase)
-            if phase + 1 < len(bits):
+            if phase + 1 < last:
                 stream.start(phase + 1)
-    key_out[...] = key_t[me]
+    leaving = [
+        pltpu.make_async_copy(key_t.at[me], key_out, in_sem.at[0]),
+        pltpu.make_async_copy(key_t.at[flip(me, last)], key_away, in_sem.at[1]),
+        pltpu.make_async_copy(query_t.at[mc], query_out, in_sem.at[2]),
+    ]
     total = small_row[0]
     for s, peer in enumerate(row_peers, 1):
         row_copy(s, peer).wait_recv()
         total = total + small_row[s]
     small_out[...] = total
+    for copy in leaving:
+        copy.start()
     for copy in sent:
         copy.wait_send()
+    for copy in leaving:
+        copy.wait()
     for stream in streams:
         stream.drain()
-    for i in range(max(blocks - 2, 0), blocks):
+
+    def end_copy(i, carry):
         a_copy(i).wait()
-
-
-def pair_kernel(block, a_in, scaled, gpair, pg_out):
-    w_hi, w_lo = split2(scaled[...])
+        return carry
+
+    lax.fori_loop(0, blocks, end_copy, 0)
+
+
+def pair_kernel(block, scale, a_in, bias_in, gpair, pg_out):
+    heads, channels = bias_in.shape
+    w_hi, w_lo = split2(
+        jnp.concatenate(
+            [scale * bias_in[...].astype(F32), jnp.zeros((PAD - heads, channels), F32)], 0
+        )
+    )
     for r in range(block):
-        a = a_in[r]
+        step = 2 * PAD
+        a = jnp.concatenate(
+            [a_in[r, at : at + step, :] for at in range(0, a_in.shape[1], step)], 1
+        )
         lhs = jnp.concatenate([a, a[:PAD]], 0)
         rhs = jnp.concatenate([w_hi, gpair[r], w_lo], 0)
         pg_out[r] = dot(lhs, rhs, TN).astype(BF16)
 
 
-def turn(rotation, local):
-    return jnp.sum(rotation[:, :, None, :] * local[None], axis=1)
-
-
-def turn_back(rotation, vector):
-    return jnp.sum(rotation[:, :, None, :] * vector[:, None], axis=0)
-
-
-def frame_terms(grad_global, local):
-    rotation_part = jnp.sum(grad_global[:, None] * local[None], axis=2)
-    return jnp.concatenate([rotation_part, jnp.sum(grad_global, axis=1)[:, None, :]], axis=1)
-
-
-def by_head(x, heads):
-    points = x.shape[1] // heads
-    return x.reshape(3, heads, points, -1).transpose(1, 0, 2, 3).reshape(heads, 3 * points, -1)
-
-
-def by_axis(x):
-    heads, rows, m = x.shape
-    return x.reshape(heads, 3, rows // 3, m).transpose(1, 0, 2, 3).reshape(3, heads * rows // 3, m)
+def own_lanes(load, start, size, total):
+    if total == size:
+        return load(slice(None))
+    first = pl.multiple_of((start // 128) * 128, 128)
+    tile = load(pl.ds(first, 128))
+    return pltpu.roll(tile, lax.rem(128 - lax.rem(start, 128), 128), 1)[:, :size]
+
+
+def upright(ref, rows):
+    for t in range(rows.shape[0] // 128):
+        part = slice(128 * t, 128 * t + 128)
+        rows[part, :] = ref(part).T
+
+
+def tail_kernel(
+    shape, key_own, key_more, query_part, small, head_w, rot, shift, query_points, grad_points,
+    key_points, value_points,
+    query_grad, query_point_grad, query_frame, key_grad, value_grad, key_point_grad,
+    value_point_grad, key_frame, weight_total, head_grad,
+    krows, qrows, dpoint, dvalue, wide,
+):
+    heads, scale, inner, point_factor, nq, nv, vwidth, qsize = shape
+    qpoints, vpoints = (qsize - vwidth) // 3, (nv - vwidth) // 3
+    me = lax.axis_index("row")
+    mc = lax.axis_index("col")
+    coef = point_coef(head_w, point_factor)
+    weight_total[...] = small[:heads, :]
+    x = head_w[...]
+    grads = small[heads : heads + 1, :heads]
+    slope = -point_factor
+    head_grad[...] = grads * slope / (1.0 + jnp.exp(-x))
+
+    def flat(source, out):
+        rows = source.shape[0]
+        wide[0:rows, 0 : source.shape[1]] = source
+        for t in range(wide.shape[0] // 128):
+            piece = wide[128 * t : 128 * t + 128, :].T
+            end = min(128, rows - 128 * t)
+            if end > 0:
+                out(slice(128 * t, 128 * t + end), piece[: source.shape[1], :end])
+
+    wide[...] = jnp.zeros_like(wide)
+
+    def put(ref):
+        def store(lanes, value):
+            ref[:, lanes] = value
+
+        return store
+
+    share = query_part.shape[0]
+    upright(lambda part: query_part[:, part], qrows)
+    start = mc * share
+    base = me * (share * lax.axis_size("col")) + start
+    total = rot.shape[2]
+    turns = [
+        [own_lanes(lambda s: rot[i, j : j + 1, s], base, share, total) for j in range(3)]
+        for i in range(3)
+    ]
+    shifts = [own_lanes(lambda s: shift[i : i + 1, s], base, share, total) for i in range(3)]
+    local = [
+        own_lanes(lambda s: query_points[y, :, s], start, share, query_points.shape[2])
+        for y in range(3)
+    ]
+    cotan = [
+        own_lanes(lambda s: grad_points[y, :, s], start, share, grad_points.shape[2])
+        for y in range(3)
+    ]
+    nr = nq + nv - vwidth
+    flat(
+        (scale * inner)
+        * jnp.concatenate([qrows[nr * h : nr * h + vwidth] for h in range(heads)], 0),
+        put(query_grad),
+    )
+    spin = lambda i, v: turns[i][0] * v[0] + turns[i][1] * v[1] + turns[i][2] * v[2]
+    for i in range(3):
+        qg = spin(i, local) + shifts[i]
+        for h in range(heads):
+            points = slice(qpoints * h, qpoints * h + qpoints)
+            at = nr * h + vwidth + qpoints * i
+            sums = qrows[nr * h + qsize + 1 : nr * h + qsize + 2]
+            dpoint[i, points] = (-2.0 * pick_lane(coef, h)) * (
+                qg[points] * sums - qrows[at : at + qpoints]
+            )
+            at = nr * h + nq + vpoints * i
+            dvalue[i, vpoints * h : vpoints * h + vpoints] = qrows[at : at + vpoints]
+    down = lambda v: jnp.sum(v, axis=0, keepdims=True)
+    for y in range(3):
+        query_point_grad[y] = (
+            turns[0][y] * dpoint[0] + turns[1][y] * dpoint[1] + turns[2][y] * dpoint[2]
+        )
+    for i in range(3):
+        away = dvalue[i] - shifts[i]
+        for y in range(3):
+            query_frame[i, y : y + 1] = down(dpoint[i] * local[y]) + down(away * cotan[y])
+        query_frame[i, 3:4] = down(dpoint[i]) - down(spin(i, cotan))
+
+    share = key_own.shape[0]
+    upright(lambda part: key_own[:, part] + key_more[:, part], krows)
+    start = me * share
+    base = mc * (share * lax.axis_size("row")) + start
+    turns = [
+        [own_lanes(lambda s: rot[i, j : j + 1, s], base, share, total) for j in range(3)]
+        for i in range(3)
+    ]
+    shifts = [own_lanes(lambda s: shift[i : i + 1, s], base, share, total) for i in range(3)]
+    local = [
+        own_lanes(lambda s: key_points[y, :, s], start, share, key_points.shape[2])
+        for y in range(3)
+    ]
+    values = [
+        own_lanes(lambda s: value_points[y, :, s], start, share, value_points.shape[2])
+        for y in range(3)
+    ]
+    nk = nq + nv
+    flat(jnp.concatenate([krows[nk * h : nk * h + vwidth] for h in range(heads)], 0), put(key_grad))
+    flat(
+        jnp.concatenate([krows[nk * h + nq : nk * h + nq + vwidth] for h in range(heads)], 0),
+        put(value_grad),
+    )
+    for i in range(3):
+        kg = spin(i, local) + shifts[i]
+        for h in range(heads):
+            points = slice(qpoints * h, qpoints * h + qpoints)
+            at = nk * h + vwidth + qpoints * i
+            sums = krows[nk * h + qsize : nk * h + qsize + 1]
+            dpoint[i, points] = krows[at : at + qpoints] + 2.0 * kg[points] * sums
+            at = nk * h + nq + vwidth + vpoints * i
+            dvalue[i, vpoints * h : vpoints * h + vpoints] = krows[at : at + vpoints]
+    for y in range(3):
+        key_point_grad[y] = (
+            turns[0][y] * dpoint[0] + turns[1][y] * dpoint[1] + turns[2][y] * dpoint[2]
+        )
+        flat(
+            turns[0][y] * dvalue[0] + turns[1][y] * dvalue[1] + turns[2][y] * dvalue[2],
+            put(value_point_grad.at[y]),
+        )
+    for i in range(3):
+        for y in range(3):
+            key_frame[i, y : y + 1] = down(dpoint[i] * local[y]) + down(dvalue[i] * values[y])
+        key_frame[i, 3:4] = down(dpoint[i]) + down(dvalue[i])
 
 
 def pad_rows(x, rows):
@@ -437,74 +685,51 @@
     logit_scale = math.sqrt(1.0 / 3.0)
     point_scale = math.sqrt(2.0 / (9.0 * qpoints))
     inner_scale = 1.0 / math.sqrt(width)
-    coef = 0.5 * logit_scale * point_scale * jax.nn.softplus(head_weight)
-    row_start = lax.axis_index("row") * n_rows
-    col_start = lax.axis_index("col") * n_cols
-    rot_rows = lax.dynamic_slice_in_dim(rotations, row_start, n_rows, 2)
-    shift_rows = lax.dynamic_slice_in_dim(translations, row_start, n_rows, 1)
-    rot_cols = lax.dynamic_slice_in_dim(rotations, col_start, n_cols, 2)
-    shift_cols = lax.dynamic_slice_in_dim(translations, col_start, n_cols, 1)
-    qg = by_head(turn(rot_rows, query_points) + shift_rows[:, None, :], heads)
-    kg = by_head(turn(rot_cols, key_points) + shift_cols[:, None, :], heads)
-    vg = by_head(turn(rot_cols, value_points) + shift_cols[:, None, :], heads)
-    grad_flat = turn(rot_rows, grad_points)
-    gg = by_head(grad_flat, heads)
-    q = queries.reshape(heads, width, n_rows)
-    k = key_vectors.reshape(heads, width, n_cols)
+    point_factor = 0.5 * logit_scale * point_scale
     qsize = width + 3 * qpoints
     nq = -(-(qsize + 2) // 16) * 16
     nv = width + 3 * vpoints
-    nvp = -(-nv // 16) * 16
-    c3 = coef[:, None, None]
-    q_square = jnp.sum(qg * qg, axis=1, keepdims=True)
-    k_square = jnp.sum(kg * kg, axis=1, keepdims=True)
-    qcat = pad_rows(
-        jnp.concatenate(
-            [
-                logit_scale * inner_scale * q,
-                2.0 * c3 * qg,
-                jnp.broadcast_to(-c3, (heads, 1, n_rows)),
-                -c3 * q_square,
-            ],
-            axis=1,
-        ),
-        nq,
-    )
-    kcat = pad_rows(
-        jnp.concatenate([k, kg, k_square, jnp.ones((heads, 1, n_cols), F32)], axis=1), nq
-    )
-    gcat = pad_rows(
-        jnp.concatenate([grad_output.reshape(heads, width, n_rows), gg], axis=1), nvp
-    )
-    vcat = pad_rows(jnp.concatenate([values.reshape(heads, width, n_cols), vg], axis=1), nvp)
-    w_t = jnp.pad(bias_weight.T, ((0, PAD - heads), (0, 0)))
-    scaled = logit_scale * w_t.astype(F32)
+    bias_t = bias_weight.T
     gpair = pad_rows(grad_pair, PAD)
-    limit = residue_count - col_start
+    head_row = head_weight.reshape(1, heads)
 
     block = 8
+    depth = n_cols // 128 * 2 * PAD
     rows_dev = lax.axis_size("row")
     cols_dev = lax.axis_size("col")
-    qraw = pad_rows(jnp.concatenate([qg, q_square], axis=1), PAD)
     nk = nq + nv
     nr = nq + nv - width
     key_lanes = -(-heads * nk // 128) * 128
     query_lanes = -(-heads * nr // 128) * 128
-    cut = -(-key_lanes // 256) * 128
     kshare = n_cols // rows_dev
     qshare = n_rows // cols_dev
+    slot_count = max(rows_dev - 2, 1)
+    if kshare % 16 == 0:
+        slot_shapes = [(slot_count, kshare // 2, key_lanes)] * 2
+    else:
+        cut = -(-key_lanes // 256) * 128
+        slot_shapes = [(slot_count, kshare, c) for c in (cut, key_lanes - cut)]
+    rot_rows, shift_rows = rotations, translations
+    if n_rows % 128:
+        row_start = lax.axis_index("row") * n_rows
+        rot_rows = lax.dynamic_slice_in_dim(rotations, row_start, n_rows, 2)
+        shift_rows = lax.dynamic_slice_in_dim(translations, row_start, n_rows, 1)
     vmem = pl.BlockSpec(memory_space=pltpu.VMEM)
     anywhere = pl.BlockSpec(memory_space=pl.ANY)
     sems = lambda count: pltpu.SemaphoreType.DMA((max(count, 1),))
-    a_all, key_part, query_part, small = pl.pallas_call(
+    a_all, key_own, key_away, query_part, small = pl.pallas_call(
         functools.partial(
             main_kernel,
-            (heads, block, logit_scale, rows_dev, cols_dev, nq, nv, width, qsize),
+            (
+                heads, block, logit_scale, inner_scale, point_factor, rows_dev, cols_dev,
+                nq, nv, width, qsize,
+            ),
         ),
-        in_specs=[pl.BlockSpec(memory_space=pltpu.SMEM), anywhere] + [vmem] * 7,
-        out_specs=[anywhere, vmem, vmem, vmem],
+        in_specs=[pl.BlockSpec(memory_space=pltpu.SMEM), anywhere] + [vmem] * 11 + [anywhere] * 4,
+        out_specs=[anywhere] * 4 + [vmem],
         out_shape=[
-            jax.ShapeDtypeStruct((n_rows, 2 * PAD, n_cols), BF16),
+            jax.ShapeDtypeStruct((n_rows, depth, 128), BF16),
+            jax.ShapeDtypeStruct((kshare, key_lanes), F32),
             jax.ShapeDtypeStruct((kshare, key_lanes), F32),
             jax.ShapeDtypeStruct((qshare, query_lanes), F32),
             jax.ShapeDtypeStruct((PAD, channels), F32),
@@ -518,17 +743,23 @@
             pltpu.VMEM((2, n_rows, 128), F32),
             pltpu.VMEM((key_lanes, n_cols), F32),
             pltpu.VMEM((rows_dev, kshare, key_lanes), F32),
-            pltpu.VMEM((rows_dev - 1, kshare, cut), F32),
-            pltpu.VMEM((rows_dev - 1, kshare, key_lanes - cut), F32),
+            pltpu.VMEM(slot_shapes[0], F32),
+            pltpu.VMEM(slot_shapes[1], F32),
             pltpu.VMEM((query_lanes, n_rows), F32),
             pltpu.VMEM((cols_dev, qshare, query_lanes), F32),
             pltpu.VMEM((max(cols_dev - 1, 1), qshare, query_lanes), F32),
             pltpu.VMEM((PAD, channels), F32),
             pltpu.VMEM((max(cols_dev - 1, 1), PAD, channels), F32),
             pltpu.VMEM((rows_dev, PAD, channels), F32),
-            pltpu.VMEM((2, block, 2 * PAD, n_cols), BF16),
+            pltpu.VMEM((PAD, channels), BF16),
+            pltpu.VMEM((heads, nq, n_rows), F32),
+            pltpu.VMEM((heads, nq, n_cols), F32),
+            pltpu.VMEM((heads, nv, n_rows), F32),
+            pltpu.VMEM((heads, nv, n_cols), F32),
+            pltpu.VMEM((heads, PAD, n_rows), F32),
             sems(n_rows // block),
-            sems(2),
+            sems(n_rows // block),
+            sems(4),
             sems(cols_dev),
             sems(cols_dev),
             sems(rows_dev - 1),
@@ -545,62 +776,77 @@
         compiler_params=pltpu.CompilerParams(
             collective_id=0, has_side_effects=True, vmem_limit_bytes=VMEM_LIMIT
         ),
-    )(limit, pair_rep, w_t, gpair, qcat, kcat, gcat, vcat, qraw)
-
-    out_block = 8
+    )(
+        residue_count, pair_rep, bias_t, gpair, head_row, queries, query_points, grad_output,
+        grad_points, rot_rows, shift_rows, rotations, translations,
+        key_vectors.reshape(heads, width, n_cols), values.reshape(heads, width, n_cols),
+        key_points.reshape(-1, n_cols), value_points.reshape(-1, n_cols),
+    )
+    half = rows_dev // 2
+    key_more = lax.ppermute(key_away, "row", [(i, (i + half) % rows_dev) for i in range(rows_dev)])
+
+    out_block = 16
     pair_grad = pl.pallas_call(
-        functools.partial(pair_kernel, out_block),
+        functools.partial(pair_kernel, out_block, logit_scale),
         grid=(n_rows // out_block,),
         in_specs=[
-            pl.BlockSpec((out_block, 2 * PAD, n_cols), lambda i: (i, 0, 0)),
-            pl.BlockSpec((PAD, channels), lambda i: (0, 0)),
+            pl.BlockSpec((out_block, depth, 128), lambda i: (i, 0, 0)),
+            pl.BlockSpec((heads, channels), lambda i: (0, 0)),
             pl.BlockSpec((out_block, PAD, channels), lambda i: (i, 0, 0)),
         ],
         out_specs=pl.BlockSpec((out_block, n_cols, channels), lambda i: (i, 0, 0)),
         out_shape=jax.ShapeDtypeStruct(pair_rep.shape, BF16),
         compiler_params=pltpu.CompilerParams(dimension_semantics=("arbitrary",)),
-    )(a_all, scaled, gpair)
-
-    key_sum = key_part.T[: heads * nk].reshape(heads, nk, kshare)
-    query_sum = query_part.T[: heads * nr].reshape(heads, nr, qshare)
-    weight_total = small[:heads].T
-    head_weight_grad = (
-        small[heads, :heads] * (-0.5 * logit_scale * point_scale) * jax.nn.sigmoid(head_weight)
+        cost_estimate=pl.CostEstimate(
+            flops=4 * n_rows * n_cols * channels * PAD,
+            bytes_accessed=2 * n_rows * n_cols * (channels + 2 * PAD),
+            transcendentals=0,
+        ),
+    )(a_all, bias_t, gpair)
+
+    local_q, local_g = query_points, grad_points
+    if n_rows % 128:
+        start = lax.axis_index("col") * qshare
+        local_q = lax.dynamic_slice_in_dim(query_points, start, qshare, 2)
+        local_g = lax.dynamic_slice_in_dim(grad_points, start, qshare, 2)
+    most = max(kshare, qshare, 128)
+    f32 = lambda *dims: jax.ShapeDtypeStruct(dims, F32)
+    (
+        query_grad, query_point_grad, query_frame_grad, key_grad, value_grad, key_point_grad,
+        value_point_grad, key_frame_grad, weight_total, head_weight_grad,
+    ) = pl.pallas_call(
+        functools.partial(
+            tail_kernel,
+            (heads, logit_scale, inner_scale, point_factor, nq, nv, width, qsize),
+        ),
+        in_specs=[vmem] * 11,
+        out_specs=[vmem] * 10,
+        out_shape=[
+            f32(qshare, heads * width),
+            f32(3, heads * qpoints, qshare),
+            f32(3, 4, qshare),
+            f32(kshare, heads * width),
+            f32(kshare, heads * width),
+            f32(3, heads * qpoints, kshare),
+            f32(3, kshare, heads * vpoints),
+            f32(3, 4, kshare),
+            f32(heads, channels),
+            f32(1, heads),
+        ],
+        scratch_shapes=[
+            pltpu.VMEM((key_lanes, kshare), F32),
+            pltpu.VMEM((query_lanes, qshare), F32),
+            pltpu.VMEM((3, heads * qpoints, kshare), F32),
+            pltpu.VMEM((3, heads * vpoints, kshare), F32),
+            pltpu.VMEM((-(-heads * width // 128) * 128, most), F32),
+        ],
+    )(
+        key_own, key_more, query_part, small, head_row, rotations, translations, local_q,
+        local_g, key_points, value_points,
     )
-
-    share = query_sum.shape[2]
-    start = lax.axis_index("col") * share
-    own_rows = lambda x: lax.dynamic_slice_in_dim(x, start, share, x.ndim - 1)
-    rot_own = own_rows(rot_rows)
-    shift_own = own_rows(shift_rows)
-    query_grad = (logit_scale * inner_scale * query_sum[:, :width]).reshape(heads * width, share)
-    dqg = by_axis(
-        -2.0 * c3 * (own_rows(qg) * query_sum[:, qsize + 1][:, None] - query_sum[:, width:qsize])
-    )
-    point_out = by_axis(query_sum[:, nq:])
-    query_point_grad = turn_back(rot_own, dqg)
-    cotan_own = own_rows(grad_points)
-    out_part = jnp.sum((point_out - shift_own[:, None, :])[:, None] * cotan_own[None], axis=2)
-    out_part = jnp.concatenate(
-        [out_part, -jnp.sum(own_rows(grad_flat), axis=1)[:, None, :]], axis=1
-    )
-    query_frame_grad = frame_terms(dqg, own_rows(query_points)) + out_part
-
-    kshare = key_sum.shape[2]
-    kstart = lax.axis_index("row") * kshare
-    own_cols = lambda x: lax.dynamic_slice_in_dim(x, kstart, kshare, x.ndim - 1)
-    rot_keys = own_cols(rot_cols)
-    key_grad = key_sum[:, :width].reshape(heads * width, kshare)
-    value_grad = key_sum[:, nq : nq + width].reshape(heads * width, kshare)
-    dkg = by_axis(
-        key_sum[:, width:qsize] + 2.0 * own_cols(kg) * key_sum[:, qsize][:, None]
-    )
-    dvg = by_axis(key_sum[:, nq + width :])
-    key_point_grad = turn_back(rot_keys, dkg)
-    value_point_grad = turn_back(rot_keys, dvg)
-    key_frame_grad = frame_terms(dkg, own_cols(key_points)) + frame_terms(
-        dvg, own_cols(value_points)
-    )
+    query_grad, key_grad, value_grad = query_grad.T, key_grad.T, value_grad.T
+    value_point_grad = value_point_grad.transpose(0, 2, 1)
+    weight_total, head_weight_grad = weight_total.T, head_weight_grad.reshape(heads)
     return (
         pair_grad, query_grad, query_point_grad, query_frame_grad, key_grad, value_grad,
         key_point_grad, value_point_grad, key_frame_grad, weight_total, head_weight_grad,

time: 139 us -> 95.8 us (0.69)
  local copies, waits for them, and re-layouts: 21.7 us -> 2.88 us
  other arithmetic: 15.6 us -> 0 us
  Pallas kernels: 98.1 us -> 89.1 us
  starting transfers between devices: 0 us -> 2 us
    dynamic_slice x11 -> x0, local copies, waits for them, and re-layouts: 10.6 us -> none  [the longest x4 3.91 us: per_device(): own_cols = lambda x: lax.dynamic_slice_in_dim(x, kstart, kshare, x.ndim - 1)]
    pallas_call x1, Pallas kernels: 77.5 us -> 69 us  [per_device(): pl.pallas_call(functools.partial(main_kernel, (heads, block, logit_scale,...]
    mul x10 -> x0, other arithmetic: 4.93 us -> none  [the longest x2 2.19 us: per_device(): -2.0 * c3]
    concatenate x5 -> x0, other arithmetic: 4.05 us -> none  [the longest x1 1.69 us: per_device(): jnp.concatenate([values.reshape(heads, width, n_cols), vg], axis=1)]
    reduce_sum x13 -> x0, other arithmetic: 3.62 us -> none  [the longest x2 1.55 us: frame_terms(): rotation_part = jnp.sum(grad_global[:, None] * local[None], axis=2)]
    add x3 -> x0, other arithmetic: 2.2 us -> none  [the longest x1 0.99 us: per_device(): key_sum[:, width:qsize] + 2.0 * own_cols(kg) * key_sum[:, qsize][:, None]]
    ppermute x0 -> x1, starting transfers between devices: none -> 2 us  [per_device(): lax.ppermute(key_away, 'row', [(i, (i + half) % rows_dev) for i in range(...]
    unnamed x42 -> x3, local copies, waits for them, and re-layouts: 3.49 us -> 1.95 us
  transfers between devices with their start and end apart: 0 -> 1, of which waited for: 0 -> 0; matrix products, arithmetic and copies ran while one was open for 0% -> 0% of each run, Pallas kernels for 0% -> 18%
where the time goes in v2:
time: 95.8 us; the launch traced here: 95.3 us
  Pallas kernels  89.1 us (93%)
  local copies, waits for them, and re-layouts  2.88 us (3%)
  starting transfers between devices  2 us (2%)
  between operations  1.3 us (1%)
    pallas_call x1, Pallas kernels, per_device(): pl.pallas_call(functools.partial(main_kernel, (heads, block, logit_scale,...  69 us
    pallas_call x1, Pallas kernels, per_device(): pl.pallas_call(functools.partial(pair_kernel, out_block, logit_scale), gr...  16.8 us
    pallas_call x1, Pallas kernels, per_device(): pl.pallas_call(functools.partial(tail_kernel, (heads, logit_scale, inner_...  3.4 us
    ppermute x1, starting transfers between devices, per_device(): lax.ppermute(key_away, 'row', [(i, (i + half) % rows_dev) for i in range(...  2 us
    unnamed x3, local copies, waits for them, and re-layouts  1.95 us
  transfers between devices with their start and end apart: 1, of which 0 were waited for; matrix products, arithmetic and copies ran while one was open for 0% of the time, Pallas kernels for 18%

profile of v2, /device:TPU:0, one launch (start us, length us, event | category | flops | bytes accessed | tf_op | source)
XLA Modules:
  0.0 95.3 jit_solution(17086934049068264813)
XLA Ops:
  1.3 1.3 %copy.26 = bf16[128,12,128]{2,1,0:T(8,128)(2,1)S(1)} copy(bf16[128,12,128]{2,0,1:T(8,128)(2,1)} %param.29) | data formatting | bytes 786432 | tf_op args[14]
  2.6 0.9 pad.4.gpair
  3.5 69.0 %shard_map.230 = (bf16[128,256,128]{2,1,0:T(8,128)(2,1)}, f32[64,896]{1,0:T(8,128)}, f32[64,896]{1,0:T(8,128)}, f32[64,768]{1,0:T(8,128)}, f32[16,128]{1,0:T(8,128)}) custom-call(s32[1]{0:T(128)S(6)} %copy.27.limit_ref, bf16[128,1024,128]{2,1,0:T(8,128)(2,1)} %pair.1, bf16[12,128]{1,0:T(8,128)(2,1)} %bitcast.16, bf16[128,16,128]{2,1,0:T(8,128)(2,1)} %pad.4.gpair, ...), custom_call_target="tpu_custom_call" | custom-call | tf_op jit(solution)/shard_map/pallas_call | solution.py:720
  72.5 2.0 %collective-permute-start = (f32[64,896]{1,0:T(8,128)}, f32[64,896]{1,0:T(8,128)S(1)}, u32[]{:S(2)}, u32[]{:S(2)}) collective-permute-start(f32[64,896]{1,0:T(8,128)} %get-tuple-element.28), channel_id=1, source_target_pairs={{0,16},{2,18},{4,20},{6,22},{8,24},{10,26},{12,28},{14,30},{16,0},... | collective-permute-start | bytes 688136 | tf_op jit(solution)/shard_map/ppermute | solution.py:786
  74.5 16.8 %shard_map.231 = bf16[128,1024,128]{2,1,0:T(8,128)(2,1)} custom-call(bf16[128,256,128]{2,1,0:T(8,128)(2,1)} %get-tuple-element.26.a_in, bf16[12,128]{1,0:T(8,128)(2,1)} %bitcast.17, bf16[128,16,128]{2,1,0:T(8,128)(2,1)} %pad.4.gpair), custom_call_target="tpu_custom_call" | custom-call | flops 1073741824 | bytes 41943040 | tf_op jit(solution)/shard_map/pallas_call | solution.py:789
  91.2 0.0 collective-permute-done.key_more
  91.2 0.0 copy-start
  91.2 0.7 copy-done
  91.9 3.4 %shard_map.232 = (f32[64,192]{1,0:T(8,128)}, f32[3,48,64]{2,1,0:T(8,128)}, f32[3,4,64]{2,1,0:T(4,128)}, f32[64,192]{1,0:T(8,128)}, f32[64,192]{1,0:T(8,128)}, /*...) custom-call(f32[64,896]{1,0:T(8,128)} %get-tuple-element.27.key_own,, ...), custom_call_target="tpu_custom_call" | custom-call | tf_op jit(solution)/shard_map/pallas_call | solution.py:817
Async XLA Ops:
  72.5 18.8 %collective-permute-start = (f32[64,896]{1,0:T(8,128)}, f32[64,896]{1,0:T(8,128)S(1)}, u32[]{:S(2)}, u32[]{:S(2)}) collective-permute-start(f32[64,896]{1,0:T(8,128)} %get-tuple-element.28), channel_id=1, source_target_pairs={{0,16},{2,18},{4,20},{6,22},{8,24},{10,26},{12,28},{14,30},{16,0},... | collective-permute-start | bytes 688136 | tf_op jit(solution)/shard_map/ppermute | solution.py:786
  91.2 0.7 copy-start

commit v3 on v2

--- a/solution.py
+++ b/solution.py
@@ -157,13 +157,13 @@
     shape, limit_ref, pair, bias_in, gpair, head_w, queries, query_points, grad_output,
     grad_points, rot_r, shift_r, rot_c, shift_c, key_in, value_in, key_points, value_points,
     a_out, key_out, key_away, query_out, small_out,
-    pair_buf, lbase, dbase, rows_buf, stats, merge_buf, key_rows, key_t, slots_a, slots_b,
+    pair_buf, lbase, dbase, rows_buf, stats, merge_buf, key_rows, key_t, slots,
     query_rows, query_t, qslots, small, small_col, small_row,
     bias_w, qcat, kcat, gcat, vcat, qraw,
-    pair_sem, a_sem, in_sem, stat_send, stat_recv, send_a, recv_a, send_b, recv_b, q_send, q_recv,
+    pair_sem, a_sem, in_sem, stat_send, stat_recv, key_send, key_recv, q_send, q_recv,
     col_send, col_recv, row_send, row_recv,
 ):
-    heads, block, scale, inner, point_factor, nr_dev, nc_dev, nq, nv, vwidth, qsize = shape
+    heads, block, scale, inner, point_factor, nr_dev, nc_dev, nq, nv, vwidth, qsize, lead = shape
     n_rows, cols = pair_buf.shape[0], pair_buf.shape[1]
     blocks = n_rows // block
     me = lax.axis_index("row")
@@ -323,7 +323,9 @@
     key_rows[...] = jnp.zeros_like(key_rows)
     query_rows[...] = jnp.zeros_like(query_rows)
 
-    def sums(h, carry):
+    lead_heads, lead_lanes = lead
+
+    def sums(shift, h, carry):
         mine = lane_of == h
         pick = lambda x: jnp.sum(jnp.where(mine, x, 0.0), axis=1, keepdims=True)
         att = lbase[h] * pick(merge_buf[0])
@@ -337,7 +339,7 @@
         kk = dot(q, d0, NN) + dot(q, d1, NN)
         vv = dot(g, a0, NN)
         half = g.shape[0] // 2
-        first = pl.multiple_of(h * (nq + nv), 8)
+        first = pl.multiple_of(h * (nq + nv) + shift, 8)
         key_rows[pl.ds(first, nq), :] = kk[:nq] + kk[nq:]
         key_rows[pl.ds(first + nq, nv), :] = vv[:nv] + vv[half : half + nv]
         qq = dot(k, d0, NT) + dot(k, d1, NT)
@@ -358,32 +360,61 @@
         )
         return carry
 
-    lax.fori_loop(0, heads, sums, 0)
-
     share = cols // nr_dev
-    for t in range(key_t.shape[2] // 128):
-        part = slice(128 * t, 128 * t + 128)
-        key_t[:, :, part] = key_rows[part, :].T.reshape(nr_dev, share, 128)
+    lane_count = key_t.shape[2]
+    bits = list(range(nr_dev.bit_length() - 1))
+    swapped = bits[:1] + bits[1:3][::-1] + bits[3:]
+    last = len(bits) - 1
+    lane_parts = [pl.ds(0, lead_lanes), pl.ds(lead_lanes, lane_count - lead_lanes)]
+    if len(slots) == 4:
+        cut = share // 2
+        halves = [(pl.ds(0, cut), bits), (pl.ds(cut, share - cut), swapped)]
+        plans = [[(half, order) for half, order in halves]] * 2
+    else:
+        plans = [[(slice(None), bits)], [(slice(None), swapped)]]
+    groups, count = [], 0
+    for lanes_of, plan in zip(lane_parts, plans):
+        group = []
+        for half, order in plan:
+            part = (half, lanes_of)
+            group.append(
+                Scatter(
+                    me, key_t, part, order, slots[count], key_send.at[count], key_recv.at[count]
+                )
+            )
+            count += 1
+        groups.append(group)
+
+    def begin(group, phase):
+        for stream in groups[group]:
+            if phase < last:
+                stream.start(phase)
+
+    def advance(group, phase):
+        for stream in groups[group]:
+            if phase < last:
+                stream.finish(phase)
+            if phase + 1 < last:
+                stream.start(phase + 1)
+
+    def upright_keys(first, end):
+        for t in range(first // 128, end // 128):
+            part = slice(128 * t, 128 * t + 128)
+            key_t[:, :, part] = key_rows[part, :].T.reshape(nr_dev, share, 128)
+
+    lax.fori_loop(0, lead_heads, functools.partial(sums, 0), 0)
+    upright_keys(0, lead_lanes)
+    begin(0, 0)
+    shift = lead_lanes - lead_heads * (nq + nv)
+    lax.fori_loop(lead_heads, heads, functools.partial(sums, shift), 0)
+    upright_keys(lead_lanes, lane_count)
+    advance(0, 0)
+    begin(1, 0)
     qshare = n_rows // nc_dev
     for t in range(query_t.shape[2] // 128):
         part = slice(128 * t, 128 * t + 128)
         query_t[:, :, part] = query_rows[part, :].T.reshape(nc_dev, qshare, 128)
 
-    bits = list(range(nr_dev.bit_length() - 1))
-    swapped = bits[:1] + bits[1:3][::-1] + bits[3:]
-    lane_count = key_t.shape[2]
-    if slots_a.shape[2] == lane_count:
-        cut = slots_a.shape[1]
-        parts = [(pl.ds(0, cut), slice(None)), (pl.ds(cut, share - cut), slice(None))]
-    else:
-        cut = slots_a.shape[2]
-        parts = [(slice(None), pl.ds(0, cut)), (slice(None), pl.ds(cut, lane_count - cut))]
-    streams = [
-        Scatter(me, key_t, parts[0], bits, slots_a, send_a, recv_a),
-        Scatter(me, key_t, parts[1], swapped, slots_b, send_b, recv_b),
-    ]
-    last = len(bits) - 1
-
     def q_copy(s, peer):
         return remote(
             query_t.at[peer], qslots.at[s], q_send.at[s], q_recv.at[s], {"col": peer}
@@ -393,10 +424,6 @@
         copy = q_copy(s, peer)
         copy.start()
         sent.append(copy)
-    for stream in streams:
-        if last > 0:
-            stream.start(0)
-
     rows_buf[...] = jnp.zeros_like(rows_buf)
 
     depth = a_out.shape[1]
@@ -432,14 +459,12 @@
 
         return carry
 
-    early = blocks // 4
+    early, middle = blocks // 4, (5 * blocks) // 8
     lax.fori_loop(0, early, weights, 0)
-    for stream in streams:
-        if last > 0:
-            stream.finish(0)
-        if last > 1:
-            stream.start(1)
-    lax.fori_loop(early, blocks, weights, 0)
+    advance(1, 0)
+    lax.fori_loop(early, middle, weights, 0)
+    advance(0, 1)
+    lax.fori_loop(middle, blocks, weights, 0)
     a_copy(blocks - 1).start()
 
     def col_copy(s, peer):
@@ -457,12 +482,6 @@
         total = total + qslots[s]
     query_t[mc] = total
 
-    for stream in streams:
-        if last > 1:
-            stream.finish(1)
-        if last > 2:
-            stream.start(2)
-
     total = small[...]
     for s, peer in enumerate(col_peers):
         col_copy(s, peer).wait_recv()
@@ -478,11 +497,10 @@
         copy = row_copy(s, peer)
         copy.start()
         sent.append(copy)
+    advance(1, 1)
     for phase in range(2, last):
-        for stream in streams:
-            stream.finish(phase)
-            if phase + 1 < last:
-                stream.start(phase + 1)
+        advance(0, phase)
+        advance(1, phase)
     leaving = [
         pltpu.make_async_copy(key_t.at[me], key_out, in_sem.at[0]),
         pltpu.make_async_copy(key_t.at[flip(me, last)], key_away, in_sem.at[1]),
@@ -499,8 +517,9 @@
         copy.wait_send()
     for copy in leaving:
         copy.wait()
-    for stream in streams:
-        stream.drain()
+    for group in groups:
+        for stream in group:
+            stream.drain()
 
     def end_copy(i, carry):
         a_copy(i).wait()
@@ -547,7 +566,7 @@
     value_point_grad, key_frame, weight_total, head_grad,
     krows, qrows, dpoint, dvalue, wide,
 ):
-    heads, scale, inner, point_factor, nq, nv, vwidth, qsize = shape
+    heads, scale, inner, point_factor, nq, nv, vwidth, qsize, lead = shape
     qpoints, vpoints = (qsize - vwidth) // 3, (nv - vwidth) // 3
     me = lax.axis_index("row")
     mc = lax.axis_index("col")
@@ -640,19 +659,20 @@
         for y in range(3)
     ]
     nk = nq + nv
-    flat(jnp.concatenate([krows[nk * h : nk * h + vwidth] for h in range(heads)], 0), put(key_grad))
+    starts = [nk * h if h < lead[0] else lead[1] + nk * (h - lead[0]) for h in range(heads)]
+    flat(jnp.concatenate([krows[at : at + vwidth] for at in starts], 0), put(key_grad))
     flat(
-        jnp.concatenate([krows[nk * h + nq : nk * h + nq + vwidth] for h in range(heads)], 0),
+        jnp.concatenate([krows[at + nq : at + nq + vwidth] for at in starts], 0),
         put(value_grad),
     )
     for i in range(3):
         kg = spin(i, local) + shifts[i]
         for h in range(heads):
             points = slice(qpoints * h, qpoints * h + qpoints)
-            at = nk * h + vwidth + qpoints * i
-            sums = krows[nk * h + qsize : nk * h + qsize + 1]
+            at = starts[h] + vwidth + qpoints * i
+            sums = krows[starts[h] + qsize : starts[h] + qsize + 1]
             dpoint[i, points] = krows[at : at + qpoints] + 2.0 * kg[points] * sums
-            at = nk * h + nq + vwidth + vpoints * i
+            at = starts[h] + nq + vwidth + vpoints * i
             dvalue[i, vpoints * h : vpoints * h + vpoints] = krows[at : at + vpoints]
     for y in range(3):
         key_point_grad[y] = (
@@ -699,16 +719,19 @@
     cols_dev = lax.axis_size("col")
     nk = nq + nv
     nr = nq + nv - width
-    key_lanes = -(-heads * nk // 128) * 128
+    fit = lambda n: -(-n * nk // 128) * 128
+    lead_heads = min(range(heads // 2, heads), key=lambda n: fit(n) + fit(heads - n))
+    lead = (lead_heads, fit(lead_heads))
+    key_lanes = fit(lead_heads) + fit(heads - lead_heads)
     query_lanes = -(-heads * nr // 128) * 128
     kshare = n_cols // rows_dev
     qshare = n_rows // cols_dev
     slot_count = max(rows_dev - 2, 1)
     if kshare % 16 == 0:
-        slot_shapes = [(slot_count, kshare // 2, key_lanes)] * 2
+        slot_shapes = [(slot_count, kshare // 2, lead[1])] * 2
+        slot_shapes += [(slot_count, kshare // 2, key_lanes - lead[1])] * 2
     else:
-        cut = -(-key_lanes // 256) * 128
-        slot_shapes = [(slot_count, kshare, c) for c in (cut, key_lanes - cut)]
+        slot_shapes = [(slot_count, kshare, c) for c in (lead[1], key_lanes - lead[1])]
     rot_rows, shift_rows = rotations, translations
     if n_rows % 128:
         row_start = lax.axis_index("row") * n_rows
@@ -722,7 +745,7 @@
             main_kernel,
             (
                 heads, block, logit_scale, inner_scale, point_factor, rows_dev, cols_dev,
-                nq, nv, width, qsize,
+                nq, nv, width, qsize, lead,
             ),
         ),
         in_specs=[pl.BlockSpec(memory_space=pltpu.SMEM), anywhere] + [vmem] * 11 + [anywhere] * 4,
@@ -743,8 +766,7 @@
             pltpu.VMEM((2, n_rows, 128), F32),
             pltpu.VMEM((key_lanes, n_cols), F32),
             pltpu.VMEM((rows_dev, kshare, key_lanes), F32),
-            pltpu.VMEM(slot_shapes[0], F32),
-            pltpu.VMEM(slot_shapes[1], F32),
+            [pltpu.VMEM(dims, F32) for dims in slot_shapes],
             pltpu.VMEM((query_lanes, n_rows), F32),
             pltpu.VMEM((cols_dev, qshare, query_lanes), F32),
             pltpu.VMEM((max(cols_dev - 1, 1), qshare, query_lanes), F32),
@@ -762,10 +784,8 @@
             sems(4),
             sems(cols_dev),
             sems(cols_dev),
-            sems(rows_dev - 1),
-            sems(rows_dev - 1),
-            sems(rows_dev - 1),
-            sems(rows_dev - 1),
+            pltpu.SemaphoreType.DMA((len(slot_shapes), slot_count)),
+            pltpu.SemaphoreType.DMA((len(slot_shapes), slot_count)),
             sems(cols_dev - 1),
             sems(cols_dev - 1),
             sems(cols_dev - 1),
@@ -817,7 +837,7 @@
     ) = pl.pallas_call(
         functools.partial(
             tail_kernel,
-            (heads, logit_scale, inner_scale, point_factor, nq, nv, width, qsize),
+            (heads, logit_scale, inner_scale, point_factor, nq, nv, width, qsize, lead),
         ),
         in_specs=[vmem] * 11,
         out_specs=[vmem] * 10,

time: 95.8 us -> 92.9 us (0.970)
  Pallas kernels: 89.1 us -> 86 us
    pallas_call x1, Pallas kernels: 69 us -> 65.8 us  [per_device(): pl.pallas_call(functools.partial(main_kernel, (heads, block, logit_scale,...]
where the time goes in v3:
time: 92.9 us; the launch traced here: 92.4 us
  Pallas kernels  86 us (93%)
  local copies, waits for them, and re-layouts  2.88 us (3%)
  starting transfers between devices  2.17 us (2%)
  between operations  1.3 us (1%)
    pallas_call x1, Pallas kernels, per_device(): pl.pallas_call(functools.partial(main_kernel, (heads, block, logit_scale,...  65.8 us
    pallas_call x1, Pallas kernels, per_device(): pl.pallas_call(functools.partial(pair_kernel, out_block, logit_scale), gr...  16.8 us
    pallas_call x1, Pallas kernels, per_device(): pl.pallas_call(functools.partial(tail_kernel, (heads, logit_scale, inner_...  3.41 us
    ppermute x1, starting transfers between devices, per_device(): lax.ppermute(key_away, 'row', [(i, (i + half) % rows_dev) for i in range(...  2.17 us
    unnamed x3, local copies, waits for them, and re-layouts  1.95 us
  transfers between devices with their start and end apart: 1, of which 0 were waited for; matrix products, arithmetic and copies ran while one was open for 0% of the time, Pallas kernels for 18%

profile of v3, /device:TPU:0, one launch (start us, length us, event | category | flops | bytes accessed | tf_op | source)
XLA Modules:
  0.0 92.4 jit_solution(11875013129362908632)
XLA Ops:
  1.3 1.3 %copy.26 = bf16[128,12,128]{2,1,0:T(8,128)(2,1)S(1)} copy(bf16[128,12,128]{2,0,1:T(8,128)(2,1)} %param.29) | data formatting | bytes 786432 | tf_op args[14]
  2.6 0.9 %pad.4.gpair = bf16[128,16,128]{2,1,0:T(8,128)(2,1)} pad(bf16[128,12,128]{2,1,0:T(8,128)(2,1)S(1)} %copy.26, bf16[]{:T(256)} %constant.2.clone.1), padding=0_0x0_4x0_0 | pad | bytes 917506 | tf_op jit(solution)/shard_map/jit(_pad)/pad | solution.py:692
  3.5 65.8 %shard_map.230 = (bf16[128,256,128]{2,1,0:T(8,128)(2,1)}, f32[64,896]{1,0:T(8,128)}, f32[64,896]{1,0:T(8,128)}, f32[64,768]{1,0:T(8,128)}, f32[16,128]{1,0:T(8,128)}) custom-call(s32[1]{0:T(128)S(6)} %copy.27.limit_ref, bf16[128,1024,128]{2,1,0:T(8,128)(2,1)} %pair.1, bf16[12,128]{1,0:T(8,128)(2,1)} %bitcast.16, bf16[128,16,128]{2,1,0:T(8,128)(2,1)} %pad.4.gpair, ...), custom_call_target="tpu_custom_call" | custom-call | tf_op jit(solution)/shard_map/pallas_call | solution.py:743
  69.3 2.2 %collective-permute-start = (f32[64,896]{1,0:T(8,128)}, f32[64,896]{1,0:T(8,128)S(1)}, u32[]{:S(2)}, u32[]{:S(2)}) collective-permute-start(f32[64,896]{1,0:T(8,128)} %get-tuple-element.28), channel_id=1, source_target_pairs={{0,16},{2,18},{4,20},{6,22},{8,24},{10,26},{12,28},{14,30},{16,0},... | collective-permute-start | bytes 688136 | tf_op jit(solution)/shard_map/ppermute | solution.py:806
  71.5 16.8 %shard_map.231 = bf16[128,1024,128]{2,1,0:T(8,128)(2,1)} custom-call(bf16[128,256,128]{2,1,0:T(8,128)(2,1)} %get-tuple-element.26.a_in, bf16[12,128]{1,0:T(8,128)(2,1)} %bitcast.17, bf16[128,16,128]{2,1,0:T(8,128)(2,1)} %pad.4.gpair), custom_call_target="tpu_custom_call" | custom-call | flops 1073741824 | bytes 41943040 | tf_op jit(solution)/shard_map/pallas_call | solution.py:809
  88.3 0.0 collective-permute-done.key_more
  88.3 0.0 copy-start
  88.3 0.7 copy-done
  89.0 3.4 %shard_map.232 = (f32[64,192]{1,0:T(8,128)}, f32[3,48,64]{2,1,0:T(8,128)}, f32[3,4,64]{2,1,0:T(4,128)}, f32[64,192]{1,0:T(8,128)}, f32[64,192]{1,0:T(8,128)}, /*...) custom-call(f32[64,896]{1,0:T(8,128)} %get-tuple-element.27.key_own,, ...), custom_call_target="tpu_custom_call" | custom-call | tf_op jit(solution)/shard_map/pallas_call | solution.py:837
Async XLA Ops:
  69.3 18.9 %collective-permute-start = (f32[64,896]{1,0:T(8,128)}, f32[64,896]{1,0:T(8,128)S(1)}, u32[]{:S(2)}, u32[]{:S(2)}) collective-permute-start(f32[64,896]{1,0:T(8,128)} %get-tuple-element.28), channel_id=1, source_target_pairs={{0,16},{2,18},{4,20},{6,22},{8,24},{10,26},{12,28},{14,30},{16,0},... | collective-permute-start | bytes 688136 | tf_op jit(solution)/shard_map/ppermute | solution.py:806
  88.3 0.7 copy-start
